TPU v7x, 16 devices: a whole 2x2x2 slice. The times are simulated.
16 devices in a mesh: data: 16 (over z, y, x, core).
Axes of the slice: x: 2, y: 2, z: 2, core: 2. Of those that a mesh axis runs over, the one named last changes fastest.
Arguments:
- x_in: bfloat16 [16, 8, 256, 2304], P('data')
- dy_out: bfloat16 [16, 8, 256, 2304], P('data')
- w_up: bfloat16 [1, 2304, 9216], P(None, 'data')
- w_down: bfloat16 [1, 9216, 2304], P(None, 'data')
Outputs:
- output 1: bfloat16 [1, 2304, 9216], P(None, 'data')
- output 2: bfloat16 [1, 9216, 2304], P(None, 'data')
- output 3: bfloat16 [16, 8, 256, 2304], P('data')
All inputs are finite; a program needn't handle non-finite values.
Results may differ from a plain program's by a relative error of at most 0.0128372.
Values are sent between devices in bfloat16 or wider.
A program may use at most 1 GiB of HBM per device.

v0:
```python
import jax
import jax.numpy as jnp
from jax import lax
from jax.sharding import PartitionSpec as P, NamedSharding


def gelu_fn(pre_act):
    return jax.nn.gelu(pre_act, approximate=True)


def fwd_layer(h_cur, w_one, w_two):
    u_pre = jnp.dot(h_cur, w_one, preferred_element_type=jnp.float32).astype(jnp.bfloat16)
    a_act = gelu_fn(u_pre.astype(jnp.float32)).astype(jnp.bfloat16)
    h_next = (h_cur.astype(jnp.float32) + jnp.dot(a_act, w_two, preferred_element_type=jnp.float32)).astype(jnp.bfloat16)
    return u_pre, a_act, h_next


def bwd_layer(h_in, u_pre, a_act, g_cur, w_one, w_two):
    contract_rows = (((0,), (0,)), ((), ()))
    contract_cols = (((1,), (1,)), ((), ()))
    d_two = lax.dot_general(a_act, g_cur, contract_rows, preferred_element_type=jnp.float32)
    da_act = lax.dot_general(g_cur, w_two, contract_cols, preferred_element_type=jnp.float32)
    _, gelu_back = jax.vjp(gelu_fn, u_pre.astype(jnp.float32))
    du_pre = gelu_back(da_act)[0].astype(jnp.bfloat16)
    d_one = lax.dot_general(h_in, du_pre, contract_rows, preferred_element_type=jnp.float32)
    up_back = lax.dot_general(du_pre, w_one, contract_cols, preferred_element_type=jnp.float32)
    g_next = (g_cur.astype(jnp.float32) + up_back).astype(jnp.bfloat16)
    return g_next, d_one, d_two


def solution(mesh):
    def device_fn(x_loc, dy_loc, w_up_sh, w_down_sh):
        n_micro, seq_count, seq_len, d_model = x_loc.shape
        layers = w_up_sh.shape[0]
        n_tokens = seq_count * seq_len
        x_mb = x_loc.reshape(n_micro, n_tokens, d_model)
        dy_mb = dy_loc.reshape(n_micro, n_tokens, d_model)

        def micro_body(acc_pair, blk_pair):
            acc_up, acc_down = acc_pair
            h_cur, g_cur = blk_pair
            saved_acts = []
            for layer_idx in range(layers):
                w_one = lax.all_gather(w_up_sh[layer_idx], "data", axis=0, tiled=True)
                w_two = lax.all_gather(w_down_sh[layer_idx], "data", axis=0, tiled=True)
                u_pre, a_act, h_next = fwd_layer(h_cur, w_one, w_two)
                saved_acts.append((h_cur, u_pre, a_act))
                h_cur = h_next
            new_up = list(acc_up)
            new_down = list(acc_down)
            for layer_idx in reversed(range(layers)):
                h_in, u_pre, a_act = saved_acts[layer_idx]
                w_one = lax.all_gather(w_up_sh[layer_idx], "data", axis=0, tiled=True)
                w_two = lax.all_gather(w_down_sh[layer_idx], "data", axis=0, tiled=True)
                g_cur, d_one, d_two = bwd_layer(h_in, u_pre, a_act, g_cur, w_one, w_two)
                part_one = lax.psum_scatter(d_one.astype(jnp.bfloat16), "data", scatter_dimension=0, tiled=True)
                part_two = lax.psum_scatter(d_two.astype(jnp.bfloat16), "data", scatter_dimension=0, tiled=True)
                new_up[layer_idx] = acc_up[layer_idx] + part_one.astype(jnp.float32)
                new_down[layer_idx] = acc_down[layer_idx] + part_two.astype(jnp.float32)
            return (tuple(new_up), tuple(new_down)), g_cur

        up_init = tuple(jnp.zeros(w_up_sh.shape[1:], jnp.float32) for layer_idx in range(layers))
        down_init = tuple(jnp.zeros(w_down_sh.shape[1:], jnp.float32) for layer_idx in range(layers))
        (acc_up, acc_down), dx_mb = lax.scan(micro_body, (up_init, down_init), (x_mb, dy_mb))
        g_up = jnp.stack([acc_one.astype(jnp.bfloat16) for acc_one in acc_up])
        g_down = jnp.stack([acc_one.astype(jnp.bfloat16) for acc_one in acc_down])
        return g_up, g_down, dx_mb.reshape(x_loc.shape)

    return jax.shard_map(device_fn, mesh=mesh, in_specs=(P("data"), P("data"), P(None, "data"), P(None, "data")), out_specs=(P(None, "data"), P(None, "data"), P("data")), check_vma=False)
```

profile of v0, /device:TPU:0, one launch (start us, length us, event | category | flops | bytes accessed | tf_op | source)
XLA Modules:
  0.0 1082.7 jit_solution(15563974862081995349)
XLA Ops:
  7.2 0.0 all-gather.7.cloned.1.call-start
  7.2 0.7 all-gather.7.cloned.1.call-update
  7.9 0.0 all-gather.5.cloned.1.call-start
  7.9 0.7 all-gather.5.cloned.1.call-update
  8.6 0.0 reduce-scatter.7.cloned.1.call-start
  8.7 164.8 %all-gather.7.cloned.1.call-done = bf16[1,2304,9216]{2,1,0:T(8,128)(2,1)} async-done(((bf16[1,144,9216]{2,1,0:T(8,128)(2,1)}), bf16[1,2304,9216]{2,1,0:T(8,128)(2,1)}) %all-gather.7.cloned.1.call-update) | async-done | bytes 42467344 | tf_op jit(solution)/shard_map/while/body/eval_jaxpr/all_gather | solution.py:44
  173.5 97.2 %fusion.22 = bf16[2048,9216]{1,0:T(8,128)(2,1)} fusion(bf16[2048,2304]{1,0:T(8,128)(2,1)} %bitcast.30, bf16[1,2304,9216]{2,1,0:T(8,128)(2,1)} %all-gather.7.cloned.1.call-done), kind=kOutput, calls=%fused_computation.28 | convolution fusion | flops 86991962112 | bytes 89653248 | tf_op jit(solution)/shard_map/while/body/eval_jaxpr/dot_general | solution.py:12
  270.7 65.5 %all-gather.5.cloned.1.call-done = bf16[1,9216,2304]{2,1,0:T(8,128)(2,1)} async-done(((bf16[1,576,2304]{2,1,0:T(8,128)(2,1)}), bf16[1,9216,2304]{2,1,0:T(8,128)(2,1)}) %all-gather.5.cloned.1.call-update) | async-done | bytes 42467344 | tf_op jit(solution)/shard_map/while/body/eval_jaxpr/all_gather | solution.py:54
  336.1 143.9 %fusion.3 = bf16[2048,9216]{1,0:T(8,128)(2,1)} fusion(bf16[2048,9216]{1,0:T(8,128)(2,1)} %fusion.22, bf16[2048,2304]{1,0:T(8,128)(2,1)} %bitcast.32, bf16[1,9216,2304]{2,1,0:T(8,128)(2,1)} %all-gather.5.cloned.1.call-done), kind=kOutput, calls=%fused_computation.8 | convolution fusion | flops 87369449472 | bytes 127401984 | tf_op jit(solution)/shard_map/while/body/eval_jaxpr/dot_general | solution.py:22
  480.0 98.1 %fusion.10 = bf16[2304,9216]{0,1:T(8,128)(2,1)} fusion(bf16[2048,9216]{1,0:T(8,128)(2,1)} %fusion.3, bf16[2048,2304]{1,0:T(8,128)(2,1)} %bitcast.31), kind=kOutput, calls=%fused_computation.17 | convolution fusion | flops 86994321408 | bytes 89653248 | tf_op jit(solution)/shard_map/while/body/eval_jaxpr/dot_general | solution.py:25
  578.1 54.7 %copy.9 = bf16[2304,9216]{1,0:T(8,128)(2,1)} copy(bf16[2304,9216]{0,1:T(8,128)(2,1)} %fusion.10) | data formatting | bytes 84934656
  632.8 0.0 reduce-scatter.7.cloned.1.call-update
  632.8 0.0 reduce-scatter.5.cloned.1.call-start
  632.9 110.6 %convolution_convert_fusion = bf16[9216,2304]{1,0:T(8,128)(2,1)} fusion(bf16[2048,2304]{1,0:T(8,128)(2,1)} %bitcast.33, bf16[2048,9216]{1,0:T(8,128)(2,1)} %fusion.22), kind=kOutput, calls=%fused_computation.15 | convolution fusion | flops 87183065088 | bytes 89653248 | tf_op jit(solution)/shard_map/while/body/eval_jaxpr/dot_general | solution.py:21
  743.4 0.0 reduce-scatter.5.cloned.1.call-update
  743.5 100.2 %add_convert_fusion = bf16[2048,2304]{1,0:T(8,128)(2,1)} fusion(bf16[2048,2304]{1,0:T(8,128)(2,1)} %bitcast.34, bf16[2048,9216]{1,0:T(8,128)(2,1)} %fusion.3, bf16[1,2304,9216]{2,1,0:T(8,128)(2,1)} %all-gather.7.cloned.1.call-done), kind=kOutput, calls=%fused_computation.29 | convolution fusion | flops 86987243520 | bytes 99090432 | tf_op jit(solution)/shard_map/while/body/eval_jaxpr/dot_general | solution.py:26
  843.7 7.8 reduce-scatter.7.cloned.1.call-done
  851.5 5.8 copy.10
  857.3 5.9 copy.8
  863.1 212.6 %reduce-scatter.5.cloned.1.call-done = bf16[576,2304]{1,0:T(8,128)(2,1)} async-done(((bf16[9216,2304]{1,0:T(8,128)(2,1)}), bf16[576,2304]{1,0:T(8,128)(2,1)}) %reduce-scatter.5.cloned.1.call-update) | async-done | bytes 2654224 | tf_op jit(solution)/shard_map/while/body/eval_jaxpr/reduce_scatter | solution.py:57
Async XLA Ops:
  7.2 166.3 %all-gather.7.cloned.1.call-start = ((), (), s32[]{:S(2)}) async-start(), calls=%async_computation.4 | async-start | bytes 45121536 | tf_op jit(solution)/shard_map/while/body/eval_jaxpr/all_gather | solution.py:44
  7.9 328.2 %all-gather.5.cloned.1.call-start = ((), (), s32[]{:S(2)}) async-start(), calls=%async_computation.3 | async-start | bytes 45121536 | tf_op jit(solution)/shard_map/while/body/eval_jaxpr/all_gather | solution.py:54
  8.6 842.8 %reduce-scatter.7.cloned.1.call-start = ((), (), s32[]{:S(2)}) async-start(), calls=%async_computation.5 | async-start | bytes 45121536
  632.8 442.9 %reduce-scatter.5.cloned.1.call-start = ((), (), s32[]{:S(2)}) async-start(), calls=%async_computation.2 | async-start | bytes 45121536 | tf_op jit(solution)/shard_map/while/body/eval_jaxpr/reduce_scatter | solution.py:57
Sparse Core Ops, SparseCore 0:
  10.2 163.2 all-gather.6
  175.7 160.3 all-gather.4
  632.9 218.4 reduce-scatter.6
  857.2 218.5 reduce-scatter.4
where the time goes:
time: 1090 us; the launch traced here: 1080 us
  matrix products  550 us (50%)
  waiting for transfers between devices  452 us (41%)
  local copies, waits for them, and re-layouts  66.4 us (6%)
  between operations  14.2 us (1%)
    reduce_scatter x1, waiting for transfers between devices, micro_body(): lax.psum_scatter(d_two.astype(jnp.bfloat16), 'data', scatter_dimension=0,...  213 us
    all_gather x1, waiting for transfers between devices, micro_body(): w_one = lax.all_gather(w_up_sh[layer_idx], 'data', axis=0, tiled=True)  165 us
    dot_general x1, matrix products, bwd_layer(): lax.dot_general(g_cur, w_two, contract_cols, preferred_element_type=jnp.f...  144 us
    dot_general x1, matrix products, bwd_layer(): lax.dot_general(a_act, g_cur, contract_rows, preferred_element_type=jnp.f...  111 us
    dot_general x1, matrix products, bwd_layer(): lax.dot_general(du_pre, w_one, contract_cols, preferred_element_type=jnp....  100 us
    dot_general x1, matrix products, bwd_layer(): lax.dot_general(h_in, du_pre, contract_rows, preferred_element_type=jnp.f...  98.1 us
    dot_general x1, matrix products, fwd_layer(): jnp.dot(h_cur, w_one, preferred_element_type=jnp.float32)  97.2 us
    unnamed x3, local copies, waits for them, and re-layouts  66.4 us
  transfers between devices with their start and end apart: 4, of which 4 were waited for; matrix products, arithmetic and copies ran while one was open for 30% of the time, Pallas kernels for 0%

commit v1 on v0

v1 whole, which is shorter than its diff:
```python
import functools
import math

import jax
import jax.numpy as jnp
from jax import lax
from jax.experimental import pallas as pl
from jax.experimental.pallas import tpu as pltpu
from jax.sharding import PartitionSpec as P

MESH = pl.DeviceIdType.MESH
F32, BF16 = jnp.float32, jnp.bfloat16
CHIPS, COLOURS, CORES = 8, 3, 2
DX_TILES = 8
UP_TILES = 8


def copy(src, dst, sem):
    return pltpu.make_async_copy(src, dst, sem)


def wait_for(ref, sem):
    pltpu.make_async_copy(ref, ref, sem).wait()


def gelu_both(u):
    scale = math.sqrt(2.0 / math.pi)
    square = u * u
    th = jnp.tanh(scale * (u + 0.044715 * (square * u)))
    cdf = 0.5 * (1.0 + th)
    slope = cdf + (0.5 * u) * (1.0 - th * th) * (scale * (1.0 + 0.134145 * square))
    return u * cdf, slope


def kernel(nc, x_hbm, dy_hbm, up_hbm, down_hbm,
           gup_hbm, gdown_hbm, dx_hbm,
           xr_hbm, dyr_hbm, upr_hbm, a1, a2, p1, p2, ra1, ra2, rb1, rb2, rc1, rc2, du_hbm, dxr_hbm,
           ag_send, ag_recv, rs_send, rs_recv, pair_send, pair_recv, dx_send, dx_recv, gup_send, gup_recv, local):
    me = lax.axis_index("data")
    core = me % 2
    bits = [(me // 2) % 2, (me // 4) % 2, (me // 8) % 2]
    partner = me + 1 - 2 * core
    near = [me + (2 << d) * (1 - 2 * bits[d]) for d in range(3)]

    tokens, width = x_hbm.shape
    both = 2 * tokens
    rows = a1.shape[3]
    fc = a1.shape[4]
    units = a2.shape[3]
    cols = a2.shape[4]
    half = up_hbm.shape[2]

    def chip(colour, m, order):
        total = 0
        for i in range(3):
            d = (colour + i) % 3
            flipped = (m >> order[i]) & 1
            total = total + (1 << d) * ((1 - bits[d]) if flipped else bits[d])
        return total

    GATHER, REDUCE = (0, 1, 2), (2, 1, 0)

    def up_rows(colour, m, order):
        return pl.ds(pl.multiple_of(chip(colour, m, order) * (3 * rows) + colour * rows, 16), rows)

    def down_rows(colour, m, order):
        return pl.ds(pl.multiple_of(chip(colour, m, order) * units, 16), units)

    def down_cols(colour):
        return pl.ds(colour * cols, cols)

    def ag_start(n, s):
        have = 1 << s
        for k in range(COLOURS):
            for buf in (a1, a2):
                pltpu.make_async_remote_copy(
                    src_ref=buf.at[n, k, pl.ds(0, have)], dst_ref=buf.at[n, k, pl.ds(have, have)],
                    send_sem=ag_send.at[s, n], recv_sem=ag_recv.at[s, n],
                    device_id=(near[(k + s) % 3],), device_id_type=MESH).start()

    sized = (rb1, ra1, p1)

    def ag_wait(n, s):
        wait_for(sized[s].at[n], ag_recv.at[s, n])

    def rs_start(n, s, k, src1, src2):
        dst1, dst2 = ((ra1, ra2), (rb1, rb2), (rc1, rc2))[s]
        for src, dst in ((src1, dst1), (src2, dst2)):
            pltpu.make_async_remote_copy(
                src_ref=src, dst_ref=dst.at[n, k], send_sem=rs_send.at[s, n], recv_sem=rs_recv.at[s, n],
                device_id=(near[(k + s) % 3],), device_id_type=MESH).start()

    def rs_wait(n, s):
        wait_for(sized[2 - s].at[n], rs_recv.at[s, n])

    barrier = pltpu.get_barrier_semaphore()
    for other in (partner, *near):
        pl.semaphore_signal(barrier, inc=1, device_id=(other,), device_id_type=MESH)
    pl.semaphore_wait(barrier, 4)

    def to_partner(src, dst, i):
        pltpu.make_async_remote_copy(
            src_ref=src, dst_ref=dst, send_sem=pair_send.at[i], recv_sem=pair_recv.at[i],
            device_id=(partner,), device_id_type=MESH).start()

    to_partner(up_hbm.at[1 - core], upr_hbm, 0)
    to_partner(x_hbm, xr_hbm, 1)
    to_partner(dy_hbm, dyr_hbm, 2)
    mine = pl.ds(pl.multiple_of(core * tokens, 16), tokens)
    theirs = pl.ds(pl.multiple_of((1 - core) * tokens, 16), tokens)

    def main(x, dy, w1, w2, ud, at, s1, s2):
        for n in range(nc):
            copy(up_hbm.at[core, n], ud.at[pl.ds(pl.multiple_of(n * 3 * rows + core * half, 16), half)], local.at[0]).start()
        own_down = x.at[pl.ds(0, nc * units)]
        copy(down_hbm, own_down, local.at[1]).start()
        wait_for(down_hbm, local.at[1])
        for n in range(nc):
            for k in range(COLOURS):
                copy(x.at[pl.ds(n * units, units), down_cols(k)], a2.at[n, k, 0], local.at[1]).start()
        wait_for(upr_hbm, pair_recv.at[0])
        for n in range(nc):
            copy(upr_hbm.at[n], ud.at[pl.ds(pl.multiple_of(n * 3 * rows + (1 - core) * half, 16), half)], local.at[0]).start()
        wait_for(up_hbm, local.at[0])
        for n in range(nc):
            for k in range(COLOURS):
                copy(ud.at[pl.ds((n * 3 + k) * rows, rows)], a1.at[n, k, 0], local.at[0]).start()
        wait_for(up_hbm, local.at[0])
        wait_for(down_hbm, local.at[1])
        ag_start(0, 0)
        copy(x_hbm, x.at[mine], local.at[1]).start()
        copy(dy_hbm, dy.at[mine], local.at[2]).start()
        ag_wait(0, 0)
        ag_start(0, 1)
        wait_for(xr_hbm, pair_recv.at[1])
        copy(xr_hbm, x.at[theirs], local.at[1]).start()
        ag_wait(0, 1)
        ag_start(0, 2)
        ag_start(1, 0)
        ag_start(2, 0)
        ag_start(3, 0)
        wait_for(dyr_hbm, pair_recv.at[2])
        copy(dyr_hbm, dy.at[theirs], local.at[2]).start()

        def load_weights(n):
            for k in range(COLOURS):
                for m in range(CHIPS):
                    copy(a1.at[n, k, m], w1.at[up_rows(k, m, GATHER)], local.at[3]).start()
                    copy(a2.at[n, k, m], w2.at[down_rows(k, m, GATHER), down_cols(k)], local.at[4]).start()

        ag_wait(0, 2)
        load_weights(0)
        wait_for(x, local.at[1])
        wait_for(dy, local.at[2])

        def send_up(n):
            for k in range(COLOURS):
                pltpu.make_async_remote_copy(
                    src_ref=p1.at[n, k, pl.ds(4, 4)], dst_ref=ra1.at[n, k], send_sem=rs_send.at[0, n],
                    recv_sem=rs_recv.at[0, n], device_id=(near[k],), device_id_type=MESH).start()

        def send_down(n):
            for k in range(COLOURS):
                pltpu.make_async_remote_copy(
                    src_ref=p2.at[n, k, pl.ds(4, 4)], dst_ref=ra2.at[n, k], send_sem=rs_send.at[0, n],
                    recv_sem=rs_recv.at[0, n], device_id=(near[k],), device_id_type=MESH).start()

        up_tile = both // UP_TILES

        def chunk(n, carry):
            wait_for(w1, local.at[3])
            wait_for(w2, local.at[4])

            def up_step(t, carry):
                at_t = pl.ds(pl.multiple_of(t * up_tile, up_tile), up_tile)
                u = jnp.dot(x[at_t, :], w1[...], preferred_element_type=F32).astype(BF16).astype(F32)
                da = lax.dot_general(dy[at_t, :], w2[...], (((1,), (1,)), ((), ())), preferred_element_type=F32)
                a, slope = gelu_both(u)
                ud[at_t, :] = (da * slope).astype(BF16)
                at[:, at_t] = a.astype(BF16).T

                @pl.when((t == 1) & (n == 0))
                def _():
                    ag_wait(1, 0)
                    ag_start(1, 1)
                    ag_wait(2, 0)
                    ag_start(2, 1)

                @pl.when((t == 1) & (n > 0))
                def _():
                    wait_for(p1.at[0], local.at[5])
                    send_up(n - 1)

                return carry

            lax.fori_loop(0, UP_TILES, up_step, 0)
            copy(ud, du_hbm.at[n], local.at[7]).start()

            @pl.when(n == 0)
            def _():
                ag_wait(1, 1)
                ag_start(1, 2)

            def down_grad(k, carry):
                part = pl.ds(pl.multiple_of(k * cols, cols), cols)
                s2[:, part] = jnp.dot(at[...], dy[:, part], preferred_element_type=F32).astype(BF16)
                return carry

            lax.fori_loop(0, 3, down_grad, 0)
            for k in range(COLOURS):
                for m in range(CHIPS):
                    copy(s2.at[down_rows(k, m, REDUCE), down_cols(k)], p2.at[n, k, m], local.at[6]).start()

            @pl.when(n + 1 < nc)
            def _():
                ag_wait(n + 1, 2)
                load_weights(n + 1)

            def up_grad(k, carry):
                part = pl.ds(pl.multiple_of(k * cols, cols), cols)
                s1[part, :] = lax.dot_general(
                    x[:, part], ud[...], (((0,), (0,)), ((), ())), preferred_element_type=F32).astype(BF16)
                return carry

            lax.fori_loop(0, 3, up_grad, 0)
            for k in range(COLOURS):
                for m in range(CHIPS):
                    copy(s1.at[up_rows(k, m, REDUCE)], p1.at[n, k, m], local.at[5]).start()

            @pl.when(n + 2 < nc)
            def _():
                ag_wait(n + 2, 1)
                ag_start(n + 2, 2)

            @pl.when(n + 3 < nc)
            def _():
                ag_wait(n + 3, 0)
                ag_start(n + 3, 1)

            @pl.when(n + 4 < nc)
            def _():
                ag_start(n + 4, 0)

            wait_for(p2.at[0], local.at[6])
            send_down(n)
            wait_for(ud, local.at[7])
            return carry

        lax.fori_loop(0, nc, chunk, 0)
        wait_for(p1.at[0], local.at[5])
        send_up(nc - 1)

    pl.run_scoped(
        main,
        pltpu.VMEM((both, width), BF16), pltpu.VMEM((both, width), BF16),
        pltpu.VMEM((width, fc), BF16), pltpu.VMEM((fc, width), BF16),
        pltpu.VMEM((both, fc), BF16), pltpu.VMEM((fc, both), BF16),
        pltpu.VMEM((width, fc), BF16), pltpu.VMEM((fc, width), BF16))

    dx_tile = both // DX_TILES
    half_tiles = DX_TILES // 2
    steps = 3 * DX_TILES
    hidden = nc * fc

    def last(w, du, out32, out16, got, res,
             c1, c2, cr1, cr2, co1, co2, d1, d2, do1, do2, e1, e2, eo1, eo2):
        def load_w(n, carry):
            for k in range(COLOURS):
                for m in range(CHIPS):
                    copy(a1.at[n, k, m], w.at[up_rows(k, m, GATHER), pl.ds(pl.multiple_of(n * fc, fc), fc)], local.at[0]).start()
            return carry

        lax.fori_loop(0, nc, load_w, 0)

        def tokens_at(q):
            later = q // half_tiles
            owner = (1 - later) * (1 - core) + later * core
            return pl.multiple_of(owner * tokens + (q % half_tiles) * dx_tile, dx_tile)

        def load_du(q):
            slot = q % 2
            for n in range(nc):
                copy(du_hbm.at[n, pl.ds(tokens_at(q), dx_tile)], du.at[slot, :, pl.ds(n * fc, fc)], local.at[1 + slot]).start()

        load_du(0)

        def own_at(q, n):
            return (pl.ds(pl.multiple_of((q % half_tiles) * dx_tile, dx_tile), dx_tile), pl.ds(pl.multiple_of(n * cols, cols), cols))

        def c_load(n):
            rs_wait(n, 0)
            copy(p1.at[n, :, pl.ds(2, 2)], c1, local.at[5]).start()
            copy(p2.at[n, :, pl.ds(2, 2)], c2, local.at[5]).start()
            copy(ra1.at[n, :, pl.ds(2, 2)], cr1, local.at[5]).start()
            copy(ra2.at[n, :, pl.ds(2, 2)], cr2, local.at[5]).start()

        def c_send(n):
            wait_for(p1.at[0], local.at[5])

            @pl.when(n > 0)
            def _():
                wait_for(sized[1].at[0], rs_send.at[1, n - 1])

            for k in range(COLOURS):
                co1[k] = (c1[k].astype(F32) + cr1[k].astype(F32)).astype(BF16)
                co2[k] = (c2[k].astype(F32) + cr2[k].astype(F32)).astype(BF16)
                rs_start(n, 1, k, co1.at[k], co2.at[k])

        def d_load(n):
            rs_wait(n, 1)
            for i, (b1, b2) in enumerate(((p1, p2), (ra1, ra2), (rb1, rb2))):
                copy(b1.at[n, :, 1], d1.at[i], local.at[6]).start()
                copy(b2.at[n, :, 1], d2.at[i], local.at[6]).start()

        def d_send(n):
            wait_for(d1, local.at[6])
            wait_for(d2, local.at[6])

            @pl.when(n > 0)
            def _():
                wait_for(sized[0].at[0], rs_send.at[2, n - 1])

            for k in range(COLOURS):
                do1[k] = (d1[0, k].astype(F32) + d1[1, k].astype(F32) + d1[2, k].astype(F32)).astype(BF16)
                do2[k] = (d2[0, k].astype(F32) + d2[1, k].astype(F32) + d2[2, k].astype(F32)).astype(BF16)
                rs_start(n, 2, k, do1.at[k], do2.at[k])

        def e_load(n):
            rs_wait(n, 2)
            for i, (b1, b2) in enumerate(((p1, p2), (ra1, ra2), (rb1, rb2))):
                copy(b1.at[n, :, 0], e1.at[i], local.at[7]).start()
                copy(b2.at[n, :, 0], e2.at[i], local.at[7]).start()
            copy(rc1.at[n], e1.at[3], local.at[7]).start()
            copy(rc2.at[n], e2.at[3], local.at[7]).start()

        keep = pl.ds(pl.multiple_of(core * half, 16), half)
        give = pl.ds(pl.multiple_of((1 - core) * half, 16), half)

        def e_wait_out(n):
            wait_for(gup_hbm.at[0, 0], local.at[8])
            wait_for(gdown_hbm.at[pl.ds(0, units)], local.at[9])
            wait_for(gup_hbm.at[0, 0], gup_send.at[n])

        def e_store(n):
            wait_for(e1, local.at[7])
            wait_for(e2, local.at[7])

            @pl.when(n > 0)
            def _():
                e_wait_out(n - 1)

            for k in range(COLOURS):
                eo1[k * rows:(k + 1) * rows, :] = (
                    e1[0, k].astype(F32) + e1[1, k].astype(F32) + e1[2, k].astype(F32) + e1[3, k].astype(F32)).astype(BF16)
                eo2[:, k * cols:(k + 1) * cols] = (
                    e2[0, k].astype(F32) + e2[1, k].astype(F32) + e2[2, k].astype(F32) + e2[3, k].astype(F32)).astype(BF16)
            copy(eo1.at[keep], gup_hbm.at[core, n], local.at[8]).start()
            copy(eo2, gdown_hbm.at[pl.ds(pl.multiple_of(n * units, 16), units)], local.at[9]).start()
            pltpu.make_async_remote_copy(
                src_ref=eo1.at[give], dst_ref=gup_hbm.at[core, n], send_sem=gup_send.at[n], recv_sem=gup_recv.at[n],
                device_id=(partner,), device_id_type=MESH).start()

        def pump(i):
            for first, every, load, finish in ((0, 1, c_load, c_send), (4, 2, d_load, d_send), (7, 2, e_load, e_store)):
                at = i - first
                n = at // every

                if every == 1:
                    @pl.when((at > 0) & (at <= nc))
                    def _(finish=finish, n=n):
                        finish(n - 1)

                    @pl.when((at >= 0) & (at < nc))
                    def _(load=load, n=n):
                        load(n)
                else:
                    @pl.when((at >= 0) & (at % 2 == 0) & (n < nc))
                    def _(load=load, n=n):
                        load(n)

                    @pl.when((at >= 0) & (at % 2 == 1) & (n < nc))
                    def _(finish=finish, n=n):
                        finish(n)

        def step(i, carry):
            q, n = i // 3, i % 3
            slot = i % 2

            @pl.when((i < steps) & (n == 0))
            def _():
                @pl.when(q + 1 < DX_TILES)
                def _():
                    load_du(q + 1)

                wait_for(du.at[0], local.at[1 + q % 2])

                @pl.when(i == 0)
                def _():
                    wait_for(w, local.at[0])

            @pl.when((i >= 3 * half_tiles) & (i < steps))
            def _():
                here = own_at(q, n)
                wait_for(dxr_hbm.at[here], dx_recv.at[i - 3 * half_tiles])
                copy(dxr_hbm.at[here], got, local.at[3]).start()
                copy(dy_hbm.at[here], res, local.at[4]).start()

            @pl.when((i >= 2) & (i < 3 * half_tiles + 2))
            def _():
                wait_for(out32.at[0], dx_send.at[i - 2])

            @pl.when((i >= 3 * half_tiles + 2) & (i < steps))
            def _():
                wait_for(out16.at[0], local.at[10 + slot])

            @pl.when(i < steps)
            def _():
                part = pl.ds(pl.multiple_of(n * cols, cols), cols)
                acc = lax.dot_general(du[q % 2], w[part, :], (((1,), (1,)), ((), ())), preferred_element_type=F32)

                out32[slot] = acc

            @pl.when(i < 3 * half_tiles)
            def _():
                pltpu.make_async_remote_copy(
                    src_ref=out32.at[slot], dst_ref=dxr_hbm.at[own_at(q, n)], send_sem=dx_send.at[i], recv_sem=dx_recv.at[i],
                    device_id=(partner,), device_id_type=MESH).start()

            @pl.when((i >= 3 * half_tiles) & (i < steps))
            def _():
                wait_for(got, local.at[3])
                wait_for(res, local.at[4])
                out16[slot] = (res[...].astype(F32) + (out32[slot] + got[...])).astype(BF16)
                copy(out16.at[slot], dx_hbm.at[own_at(q, n)], local.at[10 + slot]).start()

            pump(i)
            return carry

        lax.fori_loop(0, max(steps, 2 * nc + 7), step, 0)
        wait_for(out16.at[0], local.at[10])
        wait_for(out16.at[0], local.at[11])
        wait_for(sized[1].at[0], rs_send.at[1, nc - 1])
        wait_for(sized[0].at[0], rs_send.at[2, nc - 1])
        e_wait_out(nc - 1)

    pl.run_scoped(
        last,
        pltpu.VMEM((width, hidden), BF16), pltpu.VMEM((2, dx_tile, hidden), BF16),
        pltpu.VMEM((2, dx_tile, cols), F32), pltpu.VMEM((2, dx_tile, cols), BF16),
        pltpu.VMEM((dx_tile, cols), F32), pltpu.VMEM((dx_tile, cols), BF16),
        *[pltpu.VMEM((3, 2, *s), BF16) for _ in range(3) for s in ((rows, fc), (units, cols))],
        pltpu.VMEM((3, 3, rows, fc), BF16), pltpu.VMEM((3, 3, units, cols), BF16),
        pltpu.VMEM((3, rows, fc), BF16), pltpu.VMEM((3, units, cols), BF16),
        pltpu.VMEM((4, 3, rows, fc), BF16), pltpu.VMEM((4, 3, units, cols), BF16),
        pltpu.VMEM((3 * rows, fc), BF16), pltpu.VMEM((units, width), BF16))

    def drain(n, carry):
        for s in range(3):
            wait_for(sized[s].at[n], ag_send.at[s, n])
        wait_for(sized[2].at[n], rs_send.at[0, n])
        wait_for(gup_hbm.at[0, 0], gup_recv.at[n])
        return carry

    lax.fori_loop(0, nc, drain, 0)
    wait_for(upr_hbm, pair_send.at[0])
    wait_for(xr_hbm, pair_send.at[1])
    wait_for(dyr_hbm, pair_send.at[2])


def chunks_of(units):
    return 9 if units % 144 == 0 else 1


def solution(mesh):
    def device_fn(x_loc, dy_loc, up_loc, down_loc):
        width = x_loc.shape[-1]
        x = x_loc.reshape(-1, width)
        dy = dy_loc.reshape(-1, width)
        tokens = x.shape[0]
        down = down_loc[0]
        half, units_all = up_loc.shape[1], down.shape[0]
        nc = chunks_of(units_all)
        units = units_all // nc
        fc = CHIPS * units
        rows, cols = 2 * half // 3, width // 3
        up = up_loc.reshape(half, CHIPS, CORES, nc, units).transpose(2, 3, 0, 1, 4).reshape(CORES, nc, half, fc)

        def hbm(*shape, dtype=BF16):
            return jax.ShapeDtypeStruct(shape, dtype)

        one, two = (rows, fc), (units, cols)
        outs = [
            hbm(CORES, nc, half, fc), hbm(units_all, width), hbm(tokens, width),
            hbm(tokens, width), hbm(tokens, width), hbm(nc, half, fc),
            *[hbm(nc, 3, blocks, *s) for blocks in (8, 8, 4, 2) for s in (one, two)],
            hbm(nc, 3, *one), hbm(nc, 3, *two),
            hbm(nc, 2 * tokens, fc), hbm(tokens, width, dtype=F32),
        ]
        dma = pltpu.SemaphoreType.DMA
        half_steps = 3 * DX_TILES // 2
        got = pl.pallas_call(
            functools.partial(kernel, nc),
            out_shape=outs,
            in_specs=[pl.BlockSpec(memory_space=pl.ANY)] * 4,
            out_specs=[pl.BlockSpec(memory_space=pl.ANY)] * len(outs),
            scratch_shapes=[
                dma((3, nc)), dma((3, nc)), dma((3, nc)), dma((3, nc)), dma((3,)), dma((3,)),
                dma((half_steps,)), dma((half_steps,)), dma((nc,)), dma((nc,)), dma((12,)),
            ],
            compiler_params=pltpu.CompilerParams(
                collective_id=0, has_side_effects=True, vmem_limit_bytes=67_000_000),
        )(x, dy, up, down)
        g_up = got[0].reshape(CORES, nc, half, CHIPS, units).transpose(2, 3, 0, 1, 4).reshape(1, half, -1)
        return g_up, got[1][None], got[2].reshape(x_loc.shape)

    return jax.shard_map(
        device_fn, mesh=mesh, in_specs=(P("data"), P("data"), P(None, "data"), P(None, "data")),
        out_specs=(P(None, "data"), P(None, "data"), P("data")), check_vma=False)
```

time: 1090 us -> 674 us (0.62)
  Pallas kernels: 0 us -> 618 us
  matrix products: 550 us -> 0 us
  waiting for transfers between devices: 452 us -> 0 us
  between operations: 14.2 us -> 0.64 us
  local copies, waits for them, and re-layouts: 66.4 us -> 54.6 us
    pallas_call x0 -> x1, Pallas kernels: none -> 618 us  [device_fn(): pl.pallas_call(functools.partial(kernel, nc), out_shape=outs, in_specs=[p...]
    dot_general x5 -> x0, matrix products: 550 us -> none  [the longest x1 144 us: bwd_layer(): lax.dot_general(g_cur, w_two, contract_cols, preferred_element_type=jnp.f...]
    all_gather x2 -> x0, waiting for transfers between devices: 230 us -> none  [the longest x1 165 us: micro_body(): w_one = lax.all_gather(w_up_sh[layer_idx], 'data', axis=0, tiled=True)]
    reduce_scatter x1 -> x0, waiting for transfers between devices: 213 us -> none  [micro_body(): lax.psum_scatter(d_two.astype(jnp.bfloat16), 'data', scatter_dimension=0,...]
    unnamed x3 -> x6, local copies, waits for them, and re-layouts: 66.4 us -> 21.4 us
    transpose x0 -> x2, local copies, waits for them, and re-layouts: none -> 17.8 us  [the longest x1 9.07 us: device_fn(): got[0].reshape(CORES, nc, half, CHIPS, units).transpose(2, 3, 0, 1, 4)]
    reshape x0 -> x2, local copies, waits for them, and re-layouts: none -> 15.4 us  [the longest x1 7.91 us: device_fn(): up_loc.reshape(half, CHIPS, CORES, nc, units).transpose(2, 3, 0, 1, 4)]
  transfers between devices with their start and end apart: 4 -> 0, of which waited for: 4 -> 0; matrix products, arithmetic and copies ran while one was open for 30% -> 0% of each run, Pallas kernels for 0% -> 0%
where the time goes in v1:
time: 674 us; the launch traced here: 673 us
  Pallas kernels  618 us (92%)
  local copies, waits for them, and re-layouts  54.6 us (8%)
    pallas_call x1, Pallas kernels, device_fn(): pl.pallas_call(functools.partial(kernel, nc), out_shape=outs, in_specs=[p...  618 us
    unnamed x6, local copies, waits for them, and re-layouts  21.4 us

profile of v1, /device:TPU:0, one launch (start us, length us, event | category | flops | bytes accessed | tf_op | source)
XLA Modules:
  0.0 673.3 jit_solution(16952008904089113556)
XLA Ops:
  0.6 5.8 copy.9
  6.4 8.7 %copy.10 = bf16[2,9,144,8,64]{4,3,2,1,0:T(8,128)(2,1)} copy(bf16[2,9,144,8,64]{2,4,1,0,3:T(8,128)(2,1)} %bitcast.16) | data formatting | bytes 5308416 | tf_op jit(solution)/shard_map/transpose | solution.py:486
  15.2 7.9 %reshape.30.up_hbm = bf16[2,9,144,512]{3,2,1,0:T(8,128)(2,1)} reshape(bf16[2,9,144,8,64]{4,3,2,1,0:T(8,128)(2,1)} %copy.10) | data formatting | bytes 5308416 | tf_op jit(solution)/shard_map/reshape | solution.py:486
  23.1 618.1 %shard_map.67 = (bf16[2,9,144,512]{3,2,1,0:T(8,128)(2,1)}, bf16[576,2304]{1,0:T(8,128)(2,1)}, bf16[2048,2304]{1,0:T(8,128)(2,1)}, bf16[2048,2304]{1,0:T(8,128)(2...) custom-call(bf16[2048,2304]{1,0:T(8,128)(2,1)} %bitcast.18, ...), custom_call_target="tpu_custom_call" | custom-call | tf_op jit(solution)/shard_map/pallas_call | solution.py:501
  641.2 7.5 %reshape.31 = bf16[2,9,144,8,64]{4,3,2,1,0:T(8,128)(2,1)} reshape(bf16[2,9,144,512]{3,2,1,0:T(8,128)(2,1)} %get-tuple-element.6) | data formatting | bytes 5308416 | tf_op jit(solution)/shard_map/reshape | solution.py:513
  648.7 9.1 %copy.11 = bf16[144,8,2,9,64]{0,4,3,2,1:T(8,128)(2,1)} copy(bf16[144,8,2,9,64]{4,1,0,3,2:T(8,128)(2,1)} %bitcast.14) | data formatting | bytes 5308416 | tf_op jit(solution)/shard_map/transpose | solution.py:513
  657.8 0.0 copy-start
  657.8 6.0 copy.12
  663.8 0.0 copy-done
  663.8 1.5 copy.15
  665.3 8.0 %copy.16 = bf16[1,8,256,2304]{3,2,1,0:T(8,128)(2,1)} copy(bf16[1,8,256,2304]{3,2,1,0:T(8,128)(2,1)} %bitcast.17) | data formatting | bytes 18874368
Async XLA Ops:
  657.8 6.0 copy-start

commit v2 on v1

v2 whole, which is shorter than its diff:
```python
import functools
import math

import jax
import jax.numpy as jnp
from jax import lax
from jax.experimental import pallas as pl
from jax.experimental.pallas import tpu as pltpu
from jax.sharding import PartitionSpec as P

MESH = pl.DeviceIdType.MESH
F32, BF16 = jnp.float32, jnp.bfloat16
CHIPS, COLOURS, CORES = 8, 3, 2
DX_TILES = 8
UP_TILES = 8
PARTS = 2
UP_IN, X_IN, DY_IN, W1_IN, W2_IN, G1_OUT, G2_OUT, DU_OUT, SUM_IN, SUM_OUT, OWN_0, OWN_1, OWN_2 = range(13)
TILE_IN, _, GOT_IN, RES_IN, C_IN, D_IN, E_IN, GUP_OUT, GDOWN_OUT, DX_OUT = range(10)
EARLY = 4


def copy(src, dst, sem):
    return pltpu.make_async_copy(src, dst, sem)


def wait_for(ref, sem):
    pltpu.make_async_copy(ref, ref, sem).wait()


def gelu_both(u):
    scale = math.sqrt(2.0 / math.pi)
    square = u * u
    th = jnp.tanh(u * (scale + (0.044715 * scale) * square))
    half = 0.5 * th
    cdf = 0.5 + half
    slope = cdf + (u * (0.5 - th * half)) * (scale + (0.134145 * scale) * square)
    return u * cdf, slope


def kernel(nc, x_hbm, dy_hbm, up_hbm, down_hbm,
           gup_hbm, gdown_hbm, dx_hbm,
           xr_hbm, dyr_hbm, a1, a2, p1, p2, ra1, ra2, rb1, rb2, rc1, rc2, cb1, cb2, du_hbm, dxr_hbm,
           ag_send, ag_recv, rs_send, rs_recv, pair_send, pair_recv, dx_send, dx_recv, gup_send, gup_recv, w_sem, local):
    me = lax.axis_index("data")
    core = me % 2
    bits = [(me // 2) % 2, (me // 4) % 2, (me // 8) % 2]
    partner = me + 1 - 2 * core
    near = [me + (2 << d) * (1 - 2 * bits[d]) for d in range(3)]

    tokens, width = x_hbm.shape
    both = 2 * tokens
    rows = a1.shape[3]
    fc = a1.shape[4]
    units = a2.shape[3]
    cols = a2.shape[4]
    half = up_hbm.shape[0]
    third = half // 3

    def chip(colour, m, order):
        total = 0
        for i in range(3):
            d = (colour + i) % 3
            flipped = (m >> order[i]) & 1
            total = total + (1 << d) * ((1 - bits[d]) if flipped else bits[d])
        return total

    GATHER, REDUCE = (0, 1, 2), (2, 1, 0)

    def up_rows(colour, m, order):
        return pl.ds(pl.multiple_of(chip(colour, m, order) * (3 * rows) + colour * rows, 16), rows)

    def down_rows(colour, m, order):
        return pl.ds(pl.multiple_of(chip(colour, m, order) * units, 16), units)

    def down_cols(colour):
        return pl.ds(colour * cols, cols)

    def ag_start(n, s, arrays=(0, 1)):
        have = 1 << s
        for k in range(COLOURS):
            for i in arrays:
                buf = (a1, a2)[i]
                pltpu.make_async_remote_copy(
                    src_ref=buf.at[n, k, pl.ds(0, have)], dst_ref=buf.at[n, k, pl.ds(have, have)],
                    send_sem=ag_send.at[i, s, n], recv_sem=ag_recv.at[i, s, n],
                    device_id=(near[(k + s) % 3],), device_id_type=MESH).start()

    one_array = (rc1, rb1, ra1)
    sized = (rb1, ra1, p1)

    def ag_wait(n, s, arrays=(0, 1)):
        for i in arrays:
            wait_for(one_array[s].at[n], ag_recv.at[i, s, n])

    def rs_start(n, s, k, src1, src2):
        dst1, dst2 = ((ra1, ra2), (rb1, rb2), (rc1, rc2))[s]
        for src, dst in ((src1, dst1), (src2, dst2)):
            pltpu.make_async_remote_copy(
                src_ref=src, dst_ref=dst.at[n, k], send_sem=rs_send.at[s, n], recv_sem=rs_recv.at[s, n],
                device_id=(near[(k + s) % 3],), device_id_type=MESH).start()

    def rs_wait(n, s):
        wait_for(sized[2 - s].at[n], rs_recv.at[s, n])

    barrier = pltpu.get_barrier_semaphore()
    for other in (partner, *near):
        pl.semaphore_signal(barrier, inc=1, device_id=(other,), device_id_type=MESH)

    def to_partner(src, dst, i):
        pltpu.make_async_remote_copy(
            src_ref=src, dst_ref=dst, send_sem=pair_send.at[i], recv_sem=pair_recv.at[i],
            device_id=(partner,), device_id_type=MESH).start()

    mine = pl.ds(pl.multiple_of(core * tokens, 16), tokens)
    theirs = pl.ds(pl.multiple_of((1 - core) * tokens, 16), tokens)

    def c_load(n, c1, c2, sem):
        with jax.named_scope("wait_rs0"):
            rs_wait(n, 0)
        for i, (b1, b2) in enumerate(((p1, p2), (ra1, ra2))):
            for j in range(2):
                copy(b1.at[n, :, 2 + j], c1.at[2 * i + j], sem).start()
                copy(b2.at[n, :, 2 + j], c2.at[2 * i + j], sem).start()

    def c_sum(c1, c2, to1, to2, sem):
        wait_for(p1.at[0], sem)
        for k in range(COLOURS):
            for j in range(2):
                to1[k, j] = (c1[j, k].astype(F32) + c1[2 + j, k].astype(F32)).astype(BF16)
                to2[k, j] = (c2[j, k].astype(F32) + c2[2 + j, k].astype(F32)).astype(BF16)

    def main(x, dy, w1, w2, ud, at, s1, s2, c1, c2, co1, co2):
        own_down = x.at[pl.ds(0, nc * units)]
        blocks = up_hbm.shape[1] // width
        for b in range(blocks):
            copy(up_hbm.at[:, pl.ds(b * width, width)], x.at[pl.ds(nc * units + b * half, half)], local.at[UP_IN]).start()
        copy(down_hbm, own_down, local.at[X_IN]).start()
        wait_for(up_hbm, local.at[UP_IN])

        def unit(chip_, core_, n):
            first = ((chip_ * CORES + core_) * nc + n) * units
            b, c = first // width, first % width
            return x[nc * units + b * half:nc * units + (b + 1) * half, c:c + units]

        whole = pl.ds(pl.multiple_of(core * third, 16), 2 * third)
        rest = pl.ds(pl.multiple_of((1 - core) * 2 * third, 16), third)
        to_rest = pl.ds(pl.multiple_of(core * third, 16), third)

        def permute(n):
            for c in range(CORES):
                first = (n * CORES + c) * half
                ud[first:first + half, :] = jnp.concatenate([unit(r, c, n) for r in range(CHIPS)], axis=1)

        def own_up(n):
            def part(c, which):
                return ud.at[pl.ds(pl.multiple_of((n * CORES + c) * half + which.start, 16), which.size)]

            sem = min(n, 1)
            for which, dst in ((whole, a1.at[n, 2 * core, 0]), (rest, a1.at[n, 1, 0, to_rest])):
                pltpu.make_async_remote_copy(
                    src_ref=part(1 - core, which), dst_ref=dst, send_sem=pair_send.at[0], recv_sem=pair_recv.at[3 * sem],
                    device_id=(partner,), device_id_type=MESH).start()
                copy(part(core, which), dst, local.at[OWN_0 + sem]).start()

        def down_own(n):
            for k in range(COLOURS):
                copy(x.at[pl.ds(n * units, units), down_cols(k)], a2.at[n, k, 0], local.at[OWN_2 if n else X_IN]).start()

        permute(0)
        with jax.named_scope("entry"):
            pl.semaphore_wait(barrier, 4)
        own_up(0)
        wait_for(down_hbm, local.at[X_IN])
        down_own(0)
        for n in range(1, nc):
            permute(n)
        for n in range(1, nc):
            down_own(n)
            own_up(n)
        to_partner(x_hbm, xr_hbm, 1)
        to_partner(dy_hbm, dyr_hbm, 2)
        with jax.named_scope("own_wait"):
            wait_for(down_hbm.at[pl.ds(0, units)], local.at[X_IN])
            ag_start(0, 0, (1,))
            wait_for(du_hbm.at[0, pl.ds(0, half)], local.at[OWN_0])
            wait_for(du_hbm.at[0, pl.ds(0, half)], pair_recv.at[0])
        ag_start(0, 0, (0,))
        wait_for(down_hbm.at[pl.ds(0, (nc - 1) * units)], local.at[OWN_2])
        copy(x_hbm, x.at[mine], local.at[X_IN]).start()
        copy(dy_hbm, dy.at[mine], local.at[DY_IN]).start()
        for s in range(2):
            for i in range(2):
                with jax.named_scope(f"ag0{s}{i}"):
                    ag_wait(0, s, (i,))
                ag_start(0, s + 1, (i,))
        wait_for(du_hbm.at[0, pl.ds(0, (nc - 1) * half)], local.at[OWN_1])
        wait_for(du_hbm.at[0, pl.ds(0, (nc - 1) * half)], pair_recv.at[3])
        ag_start(1, 0)
        with jax.named_scope("xr"):
            wait_for(xr_hbm, pair_recv.at[1])
        copy(xr_hbm, x.at[theirs], local.at[X_IN]).start()

        def load_up(n):
            for k in range(COLOURS):
                for m in range(CHIPS):
                    copy(a1.at[n, k, m], w1.at[up_rows(k, m, GATHER)], local.at[W1_IN]).start()

        def load_down(n):
            for k in range(COLOURS):
                for m in range(CHIPS):
                    copy(a2.at[n, k, m], w2.at[down_rows(k, m, GATHER), down_cols(k)], local.at[W2_IN]).start()

        with jax.named_scope("ag020"):
            ag_wait(0, 2, (0,))
        load_up(0)
        with jax.named_scope("dyr"):
            wait_for(dyr_hbm, pair_recv.at[2])
        copy(dyr_hbm, dy.at[theirs], local.at[DY_IN]).start()
        with jax.named_scope("ag021"):
            ag_wait(0, 2, (1,))
        load_down(0)
        with jax.named_scope("tokens"):
            wait_for(x, local.at[X_IN])
            wait_for(dy, local.at[DY_IN])
            wait_for(du_hbm.at[0, pl.ds(0, nc * half)], pair_send.at[0])

        def send_first(src, dst, n):
            for k in range(COLOURS):
                pltpu.make_async_remote_copy(
                    src_ref=src.at[n, k, pl.ds(4, 4)], dst_ref=dst.at[n, k], send_sem=rs_send.at[0, n],
                    recv_sem=rs_recv.at[0, n], device_id=(near[k],), device_id_type=MESH).start()

        def send_both(n):
            wait_for(p2.at[0], local.at[G2_OUT])
            send_first(p2, ra2, n)
            wait_for(p1.at[0], local.at[G1_OUT])
            send_first(p1, ra1, n)

        def c_in(n):
            c_load(n, c1, c2, local.at[SUM_IN])

        def c_add(n):
            c_sum(c1, c2, co1, co2, local.at[SUM_IN])
            copy(co1, cb1.at[n], local.at[SUM_OUT]).start()
            copy(co2, cb2.at[n], local.at[SUM_OUT]).start()

        def c_go(n):
            wait_for(sized[1].at[0], local.at[SUM_OUT])
            for k in range(COLOURS):
                rs_start(n, 1, k, cb1.at[n, k], cb2.at[n, k])

        up_tile = both // UP_TILES

        def chunk(n, carry):
            with jax.named_scope("wait_w"):
                wait_for(w1, local.at[W1_IN])
                wait_for(w2, local.at[W2_IN])

            def up_step(t, carry):
                for part in range(PARTS):
                    size = up_tile // PARTS
                    first = t * up_tile + part * size
                    at_t = pl.ds(pl.multiple_of(first, size), size)
                    u = jnp.dot(x[at_t, :], w1[...], preferred_element_type=F32).astype(BF16)
                    da = lax.dot_general(dy[at_t, :], w2[...], (((1,), (1,)), ((), ())), preferred_element_type=F32)
                    strip = min(128, size)
                    for c in range(0, fc, 128):
                        for r in range(0, size, strip):
                            at_r = pl.ds(pl.multiple_of(first + r, strip), strip)
                            a, slope = gelu_both(u[r:r + strip, c:c + 128].astype(F32))
                            ud[at_r, c:c + 128] = (da[r:r + strip, c:c + 128] * slope).astype(BF16)
                            at[c:c + 128, at_r] = a.astype(BF16).T

                @pl.when((t == 1) & (n == 0))
                def _():
                    with jax.named_scope("wait_10"):
                        ag_wait(1, 0)
                    ag_start(1, 1)
                    ag_start(2, 0)

                @pl.when((t == 6) & (n == 0))
                def _():
                    with jax.named_scope("wait_11"):
                        ag_wait(1, 1)
                    ag_start(1, 2)
                    ag_start(3, 0)

                @pl.when((t == 2) & (n > 0))
                def _():
                    @pl.when(n + 1 < nc)
                    def _():
                        with jax.named_scope("wait_ag1"):
                            ag_wait(n + 1, 1)
                        ag_start(n + 1, 2)

                    @pl.when(n + 2 < nc)
                    def _():
                        with jax.named_scope("wait_ag0"):
                            ag_wait(n + 2, 0)
                        ag_start(n + 2, 1)

                    @pl.when(n + 3 < nc)
                    def _():
                        ag_start(n + 3, 0)

                    send_both(n - 1)

                @pl.when((t == 4) & (n == nc - 1))
                def _():
                    c_go(0)
                    c_add(1)
                    c_in(2)

                return carry

            with jax.named_scope("up"):
                lax.fori_loop(0, UP_TILES, up_step, 0)
            copy(ud, du_hbm.at[n], local.at[DU_OUT]).start()

            @pl.when(n == 0)
            def _():
                with jax.named_scope("wait_20"):
                    ag_wait(2, 0)
                ag_start(2, 1)

            @pl.when(n == nc - 1)
            def _():
                c_go(1)
                c_add(2)
                c_in(3)

            def down_grad(k, carry):
                part = pl.ds(pl.multiple_of(k * cols, cols), cols)
                s2[:, part] = jnp.dot(at[...], dy[:, part], preferred_element_type=F32).astype(BF16)
                return carry

            with jax.named_scope("down_grad"):
                lax.fori_loop(0, 3, down_grad, 0)
            for k in range(COLOURS):
                for m in range(CHIPS):
                    copy(s2.at[down_rows(k, m, REDUCE), down_cols(k)], p2.at[n, k, m], local.at[G2_OUT]).start()

            @pl.when(n == nc - 2)
            def _():
                c_in(0)

            @pl.when(n == nc - 1)
            def _():
                c_go(2)
                c_add(3)

            def up_grad(k, carry):
                part = pl.ds(pl.multiple_of(k * cols, cols), cols)

                @pl.when((k == 2) & (n + 1 < nc))
                def _():
                    with jax.named_scope("wait_ag2"):
                        ag_wait(n + 1, 2)
                    load_up(n + 1)
                    load_down(n + 1)

                s1[part, :] = lax.dot_general(
                    x[:, part], ud[...], (((0,), (0,)), ((), ())), preferred_element_type=F32).astype(BF16)
                return carry

            with jax.named_scope("up_grad"):
                lax.fori_loop(0, 3, up_grad, 0)
            for k in range(COLOURS):
                for m in range(CHIPS):
                    copy(s1.at[up_rows(k, m, REDUCE)], p1.at[n, k, m], local.at[G1_OUT]).start()

            @pl.when(n == nc - 2)
            def _():
                c_add(0)
                c_in(1)

            @pl.when(n == nc - 1)
            def _():
                c_go(3)

            wait_for(ud, local.at[DU_OUT])
            return carry

        lax.fori_loop(0, nc, chunk, 0)
        send_both(nc - 1)

    pl.run_scoped(
        main,
        pltpu.VMEM((both, width), BF16), pltpu.VMEM((both, width), BF16),
        pltpu.VMEM((width, fc), BF16), pltpu.VMEM((fc, width), BF16),
        pltpu.VMEM((both, fc), BF16), pltpu.VMEM((fc, both), BF16),
        pltpu.VMEM((width, fc), BF16), pltpu.VMEM((fc, width), BF16),
        pltpu.VMEM((4, 3, rows, fc), BF16), pltpu.VMEM((4, 3, units, cols), BF16),
        pltpu.VMEM((3, 2, rows, fc), BF16), pltpu.VMEM((3, 2, units, cols), BF16))

    dx_tile = both // DX_TILES
    half_tiles = DX_TILES // 2
    steps = 3 * DX_TILES
    hidden = nc * fc

    def last(w, du, out32, out16, got, res,
             co1, co2, d1, d2, do1, do2, e1, e2, eo1, eo2):
        def load_w(n, third_):
            for p in range(8):
                r, k = divmod(8 * third_ + p, 3)
                m = 0
                for i in range(3):
                    d = (k + i) % 3
                    m = m + (1 << i) * ((1 - bits[d]) if (r >> d) & 1 else bits[d])
                copy(a1.at[n, k, m], w.at[pl.ds((8 * third_ + p) * rows, rows), pl.ds(pl.multiple_of(n * fc, fc), fc)],
                     w_sem.at[third_]).start()

        def tokens_at(q):
            later = q // half_tiles
            owner = (1 - later) * (1 - core) + later * core
            return pl.multiple_of(owner * tokens + (q % half_tiles) * dx_tile, dx_tile)

        def load_du(q):
            slot = q % 2
            for n in range(nc):
                copy(du_hbm.at[n, pl.ds(tokens_at(q), dx_tile)], du.at[slot, :, pl.ds(n * fc, fc)], local.at[TILE_IN + slot]).start()

        for third_ in range(3):
            lax.fori_loop(0, nc, lambda n, carry, third_=third_: (load_w(n, third_), carry)[1], 0)
            if third_ == 0:
                load_du(0)

        def own_at(q, n):
            return (pl.ds(pl.multiple_of((q % half_tiles) * dx_tile, dx_tile), dx_tile), pl.ds(pl.multiple_of(n * cols, cols), cols))

        def c_in(n):
            c_load(n, e1, e2, local.at[C_IN])

        def c_send(n):
            to1, to2 = co1.at[n - EARLY], co2.at[n - EARLY]
            c_sum(e1, e2, to1, to2, local.at[C_IN])
            for k in range(COLOURS):
                rs_start(n, 1, k, to1.at[k], to2.at[k])

        def d_load(n):
            with jax.named_scope("wait_rs1"):
                rs_wait(n, 1)
            for i, (b1, b2) in enumerate(((p1, p2), (ra1, ra2), (rb1, rb2))):
                copy(b1.at[n, :, 1], d1.at[i], local.at[D_IN]).start()
                copy(b2.at[n, :, 1], d2.at[i], local.at[D_IN]).start()

        def d_send(n):
            wait_for(d1, local.at[D_IN])
            wait_for(d2, local.at[D_IN])

            for k in range(COLOURS):
                do1[n, k] = (d1[0, k].astype(F32) + d1[1, k].astype(F32) + d1[2, k].astype(F32)).astype(BF16)
                do2[n, k] = (d2[0, k].astype(F32) + d2[1, k].astype(F32) + d2[2, k].astype(F32)).astype(BF16)
                rs_start(n, 2, k, do1.at[n, k], do2.at[n, k])

        def e_load(n):
            with jax.named_scope("wait_rs2"):
                rs_wait(n, 2)
            for i, (b1, b2) in enumerate(((p1, p2), (ra1, ra2), (rb1, rb2))):
                copy(b1.at[n, :, 0], e1.at[i], local.at[E_IN]).start()
                copy(b2.at[n, :, 0], e2.at[i], local.at[E_IN]).start()
            copy(rc1.at[n], e1.at[3], local.at[E_IN]).start()
            copy(rc2.at[n], e2.at[3], local.at[E_IN]).start()

        keep = pl.ds(pl.multiple_of(core * half, 16), half)
        give = pl.ds(pl.multiple_of((1 - core) * half, 16), half)

        def e_wait_out(n):
            wait_for(gup_hbm.at[0, 0], local.at[GUP_OUT])
            wait_for(gdown_hbm.at[pl.ds(0, units)], local.at[GDOWN_OUT])
            wait_for(gup_hbm.at[0, 0], gup_send.at[n])

        def e_store(n):
            wait_for(e1, local.at[E_IN])
            wait_for(e2, local.at[E_IN])

            @pl.when(n > 0)
            def _():
                e_wait_out(n - 1)

            for k in range(COLOURS):
                eo1[k * rows:(k + 1) * rows, :] = (
                    e1[0, k].astype(F32) + e1[1, k].astype(F32) + e1[2, k].astype(F32) + e1[3, k].astype(F32)).astype(BF16)
                eo2[:, k * cols:(k + 1) * cols] = (
                    e2[0, k].astype(F32) + e2[1, k].astype(F32) + e2[2, k].astype(F32) + e2[3, k].astype(F32)).astype(BF16)
            copy(eo1.at[keep], gup_hbm.at[core, n], local.at[GUP_OUT]).start()
            copy(eo2, gdown_hbm.at[pl.ds(pl.multiple_of(n * units, 16), units)], local.at[GDOWN_OUT]).start()
            pltpu.make_async_remote_copy(
                src_ref=eo1.at[give], dst_ref=gup_hbm.at[core, n], send_sem=gup_send.at[n], recv_sem=gup_recv.at[n],
                device_id=(partner,), device_id_type=MESH).start()

        def pump(i):
            for start, every, low, load, finish_ in (
                    (0, 2, EARLY, c_in, c_send), (7, 1, 0, d_load, d_send), (15, 1, 0, e_load, e_store)):
                since = i - start

                @pl.when((since >= 1) & ((since - 1) % every == 0) & ((since - 1) // every < nc - low))
                def _(finish_=finish_, since=since, every=every, low=low):
                    finish_((since - 1) // every + low)

                @pl.when((since >= 0) & (since % every == 0) & (since // every < nc - low))
                def _(load=load, since=since, every=every, low=low):
                    load(since // every + low)

        def step(i, carry):
            q, n = i // 3, i % 3
            slot = i % 2

            @pl.when((i < steps) & (n == 0))
            def _():
                @pl.when(q + 1 < DX_TILES)
                def _():
                    load_du(q + 1)

                with jax.named_scope("wait_du"):
                    wait_for(du.at[0], local.at[TILE_IN + q % 2])

            @pl.when(i < 3)
            def _():
                with jax.named_scope("wait_wall"):
                    wait_for(w.at[pl.ds(0, cols)], w_sem.at[n])

            @pl.when((i >= 3 * half_tiles) & (i < steps))
            def _():
                here = own_at(q, n)
                with jax.named_scope("wait_dxr"):
                    wait_for(dxr_hbm.at[here], dx_recv.at[i - 3 * half_tiles])
                copy(dxr_hbm.at[here], got, local.at[GOT_IN]).start()
                copy(dy_hbm.at[here], res, local.at[RES_IN]).start()

            @pl.when((i >= 2) & (i < 3 * half_tiles + 2))
            def _():
                with jax.named_scope("wait_dxs"):
                    wait_for(out32.at[0], dx_send.at[i - 2])

            @pl.when((i >= 3 * half_tiles + 2) & (i < steps))
            def _():
                wait_for(out16.at[0], local.at[DX_OUT + slot])

            @pl.when(i < steps)
            def _():
                part = pl.ds(pl.multiple_of(n * cols, cols), cols)
                with jax.named_scope("dx_dot"):
                    out32[slot] = lax.dot_general(
                        du[q % 2], w[part, :], (((1,), (1,)), ((), ())), preferred_element_type=F32)

            @pl.when(i < 3 * half_tiles)
            def _():
                pltpu.make_async_remote_copy(
                    src_ref=out32.at[slot], dst_ref=dxr_hbm.at[own_at(q, n)], send_sem=dx_send.at[i], recv_sem=dx_recv.at[i],
                    device_id=(partner,), device_id_type=MESH).start()

            @pl.when((i >= 3 * half_tiles) & (i < steps))
            def _():
                wait_for(got, local.at[GOT_IN])
                wait_for(res, local.at[RES_IN])
                out16[slot] = (res[...].astype(F32) + (out32[slot] + got[...])).astype(BF16)
                copy(out16.at[slot], dx_hbm.at[own_at(q, n)], local.at[DX_OUT + slot]).start()

            pump(i)
            return carry

        lax.fori_loop(0, max(steps, nc + 16), step, 0)
        for slot in range(2):
            wait_for(out16.at[0], local.at[DX_OUT + slot])
        e_wait_out(nc - 1)
        for n in range(nc):
            wait_for(sized[1].at[0], rs_send.at[1, n])
            wait_for(sized[0].at[0], rs_send.at[2, n])

    pl.run_scoped(
        last,
        pltpu.VMEM((width, hidden), BF16), pltpu.VMEM((2, dx_tile, hidden), BF16),
        pltpu.VMEM((2, dx_tile, cols), F32), pltpu.VMEM((2, dx_tile, cols), BF16),
        pltpu.VMEM((dx_tile, cols), F32), pltpu.VMEM((dx_tile, cols), BF16),
        pltpu.VMEM((nc - EARLY, 3, 2, rows, fc), BF16), pltpu.VMEM((nc - EARLY, 3, 2, units, cols), BF16),
        pltpu.VMEM((3, 3, rows, fc), BF16), pltpu.VMEM((3, 3, units, cols), BF16),
        pltpu.VMEM((nc, 3, rows, fc), BF16), pltpu.VMEM((nc, 3, units, cols), BF16),
        pltpu.VMEM((4, 3, rows, fc), BF16), pltpu.VMEM((4, 3, units, cols), BF16),
        pltpu.VMEM((3 * rows, fc), BF16), pltpu.VMEM((units, width), BF16))

    def drain(n, carry):
        for s in range(3):
            for i in range(2):
                wait_for(one_array[s].at[n], ag_send.at[i, s, n])
        wait_for(sized[2].at[n], rs_send.at[0, n])
        wait_for(gup_hbm.at[0, 0], gup_recv.at[n])
        return carry

    with jax.named_scope("drain"):
        lax.fori_loop(0, nc, drain, 0)
    wait_for(xr_hbm, pair_send.at[1])
    wait_for(dyr_hbm, pair_send.at[2])


def finish(nc, units, gup, gdown, dx, gup_out, gdown_out, dx_out, v_in, v_out, v_down, v_dx, sem_in, sem_out):
    pieces = v_dx.shape[0]
    rows = v_dx.shape[1]
    copy(gup, v_in, sem_in.at[pieces]).start()
    copy(gdown, v_down, sem_in.at[pieces + 1]).start()
    for i in range(pieces):
        copy(dx.at[pl.ds(i * rows, rows)], v_dx.at[i], sem_in.at[i]).start()
    copy(gup, v_in, sem_in.at[pieces]).wait()
    per = 128 // math.gcd(128, units)
    for first in range(0, CHIPS * CORES * nc, per):
        parts = []
        for u in range(first, first + per):
            d, n = u // nc, u % nc
            r, c = d // CORES, d % CORES
            parts.append(v_in[c, n, :, r * units:(r + 1) * units])
        v_out[:, first * units:(first + per) * units] = jnp.concatenate(parts, axis=1)
    copy(v_out, gup_out, sem_out.at[pieces]).start()
    copy(gdown, v_down, sem_in.at[pieces + 1]).wait()
    copy(v_down, gdown_out, sem_out.at[pieces + 1]).start()
    for i in range(pieces):
        copy(dx.at[pl.ds(i * rows, rows)], v_dx.at[i], sem_in.at[i]).wait()
        copy(v_dx.at[i], dx_out.at[pl.ds(i * rows, rows)], sem_out.at[i]).start()
    copy(v_out, gup_out, sem_out.at[pieces]).wait()
    copy(v_down, gdown_out, sem_out.at[pieces + 1]).wait()
    for i in range(pieces):
        copy(v_dx.at[i], dx_out.at[pl.ds(i * rows, rows)], sem_out.at[i]).wait()


def chunks_of(units):
    return 9 if units % 144 == 0 else 1


def solution(mesh):
    def device_fn(x_loc, dy_loc, up_loc, down_loc):
        width = x_loc.shape[-1]
        x = x_loc.reshape(-1, width)
        dy = dy_loc.reshape(-1, width)
        tokens = x.shape[0]
        down = down_loc[0]
        half, units_all = up_loc.shape[1], down.shape[0]
        nc = chunks_of(units_all)
        units = units_all // nc
        fc = CHIPS * units
        rows, cols = 2 * half // 3, width // 3
        up = up_loc[0]

        def hbm(*shape, dtype=BF16):
            return jax.ShapeDtypeStruct(shape, dtype)

        one, two = (rows, fc), (units, cols)
        outs = [
            hbm(CORES, nc, half, fc), hbm(units_all, width), hbm(tokens, width),
            hbm(tokens, width), hbm(tokens, width),
            *[hbm(nc, 3, blocks, *s) for blocks in (8, 8, 4, 2) for s in (one, two)],
            hbm(nc, 3, *one), hbm(nc, 3, *two), hbm(nc, 3, 2, *one), hbm(nc, 3, 2, *two),
            hbm(nc, 2 * tokens, fc), hbm(tokens, width, dtype=F32),
        ]
        dma = pltpu.SemaphoreType.DMA
        half_steps = 3 * DX_TILES // 2
        got = pl.pallas_call(
            functools.partial(kernel, nc),
            out_shape=outs,
            in_specs=[pl.BlockSpec(memory_space=pl.ANY)] * 4,
            out_specs=[pl.BlockSpec(memory_space=pl.ANY)] * len(outs),
            scratch_shapes=[
                dma((2, 3, nc)), dma((2, 3, nc)), dma((3, nc)), dma((3, nc)), dma((3,)), dma((4,)),
                dma((half_steps,)), dma((half_steps,)), dma((nc,)), dma((nc,)), dma((3,)), dma((13,)),
            ],
            compiler_params=pltpu.CompilerParams(
                collective_id=0, has_side_effects=True, vmem_limit_bytes=67_000_000),
        )(x, dy, up, down)
        pieces = 8
        g_up, g_down, dx = pl.pallas_call(
            functools.partial(finish, nc, units),
            out_shape=[hbm(half, up.shape[1]), hbm(units_all, width), hbm(tokens, width)],
            in_specs=[pl.BlockSpec(memory_space=pl.ANY)] * 3,
            out_specs=[pl.BlockSpec(memory_space=pl.ANY)] * 3,
            scratch_shapes=[
                pltpu.VMEM((CORES, nc, half, fc), BF16), pltpu.VMEM((half, up.shape[1]), BF16),
                pltpu.VMEM((units_all, width), BF16), pltpu.VMEM((pieces, tokens // pieces, width), BF16),
                dma((pieces + 2,)), dma((pieces + 2,)),
            ],
            compiler_params=pltpu.CompilerParams(vmem_limit_bytes=67_000_000),
        )(*got[:3])
        return g_up[None], g_down[None], dx.reshape(x_loc.shape)

    return jax.shard_map(
        device_fn, mesh=mesh, in_specs=(P("data"), P("data"), P(None, "data"), P(None, "data")),
        out_specs=(P(None, "data"), P(None, "data"), P("data")), check_vma=False)
```

time: 674 us -> 571 us (0.85)
  local copies, waits for them, and re-layouts: 54.6 us -> 0 us
  Pallas kernels: 618 us -> 570 us
    pallas_call x1, Pallas kernels: 618 us -> 560 us  [device_fn(): pl.pallas_call(functools.partial(kernel, nc), out_shape=outs, in_specs=[p...]
    unnamed x6 -> x0, local copies, waits for them, and re-layouts: 21.4 us -> none
    transpose x2 -> x0, local copies, waits for them, and re-layouts: 17.8 us -> none  [the longest x1 9.07 us: device_fn(): got[0].reshape(CORES, nc, half, CHIPS, units).transpose(2, 3, 0, 1, 4)]
    reshape x2 -> x0, local copies, waits for them, and re-layouts: 15.4 us -> none  [the longest x1 7.91 us: device_fn(): up_loc.reshape(half, CHIPS, CORES, nc, units).transpose(2, 3, 0, 1, 4)]
    pallas_call x0 -> x1, Pallas kernels: none -> 10.4 us  [device_fn(): pl.pallas_call(functools.partial(finish, nc, units), out_shape=[hbm(half,...]
where the time goes in v2:
time: 571 us
  Pallas kernels  570 us (100%)
    pallas_call x1, Pallas kernels, device_fn(): pl.pallas_call(functools.partial(kernel, nc), out_shape=outs, in_specs=[p...  560 us

profile of v2, /device:TPU:0, one launch (start us, length us, event | category | flops | bytes accessed | tf_op | source)
XLA Modules:
  0.0 570.9 jit_solution(13367639295204484763)
XLA Ops:
  0.6 559.8 %shard_map.67 = (bf16[2,9,144,512]{3,2,1,0:T(8,128)(2,1)}, bf16[576,2304]{1,0:T(8,128)(2,1)}, bf16[2048,2304]{1,0:T(8,128)(2,1)}, bf16[2048,2304]{1,0:T(8,128)(2...) custom-call(bf16[2048,2304]{1,0:T(8,128)(2,1)} %bitcast.7, ...), custom_call_target="tpu_custom_call" | custom-call | tf_op jit(solution)/shard_map/pallas_call | solution.py:655
  560.4 10.4 %shard_map.68 = (bf16[144,9216]{1,0:T(8,128)(2,1)}, bf16[576,2304]{1,0:T(8,128)(2,1)}, bf16[2048,2304]{1,0:T(8,128)(2,1)}) custom-call(bf16[2,9,144,512]{3,2,1,0:T(8,128)(2,1)} %get-tuple-element.9.gup, bf16[576,2304]{1,0:T(8,128)(2,1)} %get-tuple-element.10.gdown, bf16[2048,2304]{1,0:T(8,128)(2,1)} %get-tuple-element.11.dx), custom_call_target="tpu_custom_call" | custom-call | tf_op jit(solution)/shard_map/pallas_call | solution.py:668

commit v3 on v2

--- a/solution.py
+++ b/solution.py
@@ -15,7 +15,8 @@
 UP_TILES = 8
 PARTS = 2
 UP_IN, X_IN, DY_IN, W1_IN, W2_IN, G1_OUT, G2_OUT, DU_OUT, SUM_IN, SUM_OUT, OWN_0, OWN_1, OWN_2 = range(13)
-TILE_IN, _, GOT_IN, RES_IN, C_IN, D_IN, E_IN, GUP_OUT, GDOWN_OUT, DX_OUT = range(10)
+TILE_IN, GOT_IN, RES_IN, DX_OUT = range(0, 8, 2)
+C_IN, D_IN, E_IN, GUP_OUT, GDOWN_OUT = range(8, 13)
 EARLY = 4
 
 
@@ -118,16 +119,17 @@
         with jax.named_scope("wait_rs0"):
             rs_wait(n, 0)
         for i, (b1, b2) in enumerate(((p1, p2), (ra1, ra2))):
-            for j in range(2):
-                copy(b1.at[n, :, 2 + j], c1.at[2 * i + j], sem).start()
-                copy(b2.at[n, :, 2 + j], c2.at[2 * i + j], sem).start()
+            for k in range(COLOURS):
+                pair = pl.ds(2 * (3 * i + k), 2)
+                copy(b1.at[n, k, pl.ds(2, 2)], c1.at[pair], sem).start()
+                copy(b2.at[n, k, pl.ds(2, 2)], c2.at[pair], sem).start()
 
     def c_sum(c1, c2, to1, to2, sem):
         wait_for(p1.at[0], sem)
         for k in range(COLOURS):
             for j in range(2):
-                to1[k, j] = (c1[j, k].astype(F32) + c1[2 + j, k].astype(F32)).astype(BF16)
-                to2[k, j] = (c2[j, k].astype(F32) + c2[2 + j, k].astype(F32)).astype(BF16)
+                to1[k, j] = c1[2 * k + j] + c1[2 * k + j + 6]
+                to2[k, j] = c2[2 * k + j] + c2[2 * k + j + 6]
 
     def main(x, dy, w1, w2, ud, at, s1, s2, c1, c2, co1, co2):
         own_down = x.at[pl.ds(0, nc * units)]
@@ -170,6 +172,11 @@
         with jax.named_scope("entry"):
             pl.semaphore_wait(barrier, 4)
         own_up(0)
+        for k in range(COLOURS):
+            pltpu.make_async_remote_copy(
+                src_ref=down_hbm.at[pl.ds(0, units), down_cols(k)], dst_ref=a2.at[0, k, 1],
+                send_sem=ag_send.at[1, 0, 0], recv_sem=ag_recv.at[1, 0, 0],
+                device_id=(near[k],), device_id_type=MESH).start()
         wait_for(down_hbm, local.at[X_IN])
         down_own(0)
         for n in range(1, nc):
@@ -181,7 +188,6 @@
         to_partner(dy_hbm, dyr_hbm, 2)
         with jax.named_scope("own_wait"):
             wait_for(down_hbm.at[pl.ds(0, units)], local.at[X_IN])
-            ag_start(0, 0, (1,))
             wait_for(du_hbm.at[0, pl.ds(0, half)], local.at[OWN_0])
             wait_for(du_hbm.at[0, pl.ds(0, half)], pair_recv.at[0])
         ag_start(0, 0, (0,))
@@ -213,15 +219,8 @@
         with jax.named_scope("ag020"):
             ag_wait(0, 2, (0,))
         load_up(0)
-        with jax.named_scope("dyr"):
-            wait_for(dyr_hbm, pair_recv.at[2])
-        copy(dyr_hbm, dy.at[theirs], local.at[DY_IN]).start()
-        with jax.named_scope("ag021"):
-            ag_wait(0, 2, (1,))
-        load_down(0)
         with jax.named_scope("tokens"):
             wait_for(x, local.at[X_IN])
-            wait_for(dy, local.at[DY_IN])
             wait_for(du_hbm.at[0, pl.ds(0, nc * half)], pair_send.at[0])
 
         def send_first(src, dst, n):
@@ -252,40 +251,73 @@
         up_tile = both // UP_TILES
 
         def chunk(n, carry):
-            with jax.named_scope("wait_w"):
+            size = up_tile // PARTS
+            strip = min(128, size)
+
+            def use(first, u, da):
+                for c in range(0, fc, 128):
+                    lanes = slice(c, c + 128)
+                    for r in range(0, size, strip):
+                        at_r = pl.ds(pl.multiple_of(first + r, strip), strip)
+                        a, slope = gelu_both(u(r, at_r, lanes).astype(F32))
+                        ud[at_r, lanes] = (da[r:r + strip, lanes] * slope).astype(BF16)
+                        at[lanes, at_r] = a.astype(BF16).T
+
+            def da_of(at_t):
+                return lax.dot_general(dy[at_t, :], w2[...], (((1,), (1,)), ((), ())), preferred_element_type=F32)
+
+            with jax.named_scope("wait_w1"):
                 wait_for(w1, local.at[W1_IN])
-                wait_for(w2, local.at[W2_IN])
+
+            @pl.when(n == 0)
+            def _():
+                def u_step(t, carry):
+                    at_t = pl.ds(pl.multiple_of(t * 2 * up_tile, up_tile), 2 * up_tile)
+                    ud[at_t, :] = jnp.dot(x[at_t, :], w1[...], preferred_element_type=F32).astype(BF16)
+                    return carry
+
+                with jax.named_scope("u0"):
+                    lax.fori_loop(0, UP_TILES // 2, u_step, 0)
+                with jax.named_scope("wait_100"):
+                    ag_wait(1, 0, (0,))
+                ag_start(1, 1, (0,))
+                with jax.named_scope("first_w2"):
+                    wait_for(dyr_hbm, pair_recv.at[2])
+                    copy(dyr_hbm, dy.at[theirs], local.at[DY_IN]).start()
+                    ag_wait(0, 2, (1,))
+                    load_down(0)
+                    wait_for(dy, local.at[DY_IN])
+                    wait_for(w2, local.at[W2_IN])
+
+                def da_step(t, carry):
+                    for part in range(PARTS):
+                        first = t * up_tile + part * size
+                        da = da_of(pl.ds(pl.multiple_of(first, size), size))
+                        use(first, lambda r, at_r, lanes: ud[at_r, lanes], da)
+
+                    for when, s, i in ((0, 0, 1), (3, 1, 0), (6, 1, 1)):
+                        @pl.when(t == when)
+                        def _(s=s, i=i):
+                            with jax.named_scope(f"wait_1{s}{i}"):
+                                ag_wait(1, s, (i,))
+                            ag_start(1, s + 1, (i,))
+
+                    return carry
+
+                with jax.named_scope("da0"):
+                    lax.fori_loop(0, UP_TILES, da_step, 0)
+                ag_start(2, 0)
+                ag_start(3, 0)
 
             def up_step(t, carry):
                 for part in range(PARTS):
-                    size = up_tile // PARTS
                     first = t * up_tile + part * size
                     at_t = pl.ds(pl.multiple_of(first, size), size)
                     u = jnp.dot(x[at_t, :], w1[...], preferred_element_type=F32).astype(BF16)
-                    da = lax.dot_general(dy[at_t, :], w2[...], (((1,), (1,)), ((), ())), preferred_element_type=F32)
-                    strip = min(128, size)
-                    for c in range(0, fc, 128):
-                        for r in range(0, size, strip):
-                            at_r = pl.ds(pl.multiple_of(first + r, strip), strip)
-                            a, slope = gelu_both(u[r:r + strip, c:c + 128].astype(F32))
-                            ud[at_r, c:c + 128] = (da[r:r + strip, c:c + 128] * slope).astype(BF16)
-                            at[c:c + 128, at_r] = a.astype(BF16).T
-
-                @pl.when((t == 1) & (n == 0))
-                def _():
-                    with jax.named_scope("wait_10"):
-                        ag_wait(1, 0)
-                    ag_start(1, 1)
-                    ag_start(2, 0)
-
-                @pl.when((t == 6) & (n == 0))
-                def _():
-                    with jax.named_scope("wait_11"):
-                        ag_wait(1, 1)
-                    ag_start(1, 2)
-                    ag_start(3, 0)
-
-                @pl.when((t == 2) & (n > 0))
+                    da = da_of(at_t)
+                    use(first, lambda r, at_r, lanes, u=u: u[r:r + strip, lanes], da)
+
+                @pl.when(t == 4)
                 def _():
                     @pl.when(n + 1 < nc)
                     def _():
@@ -305,7 +337,7 @@
 
                     send_both(n - 1)
 
-                @pl.when((t == 4) & (n == nc - 1))
+                @pl.when((t == 6) & (n == nc - 1))
                 def _():
                     c_go(0)
                     c_add(1)
@@ -313,15 +345,14 @@
 
                 return carry
 
-            with jax.named_scope("up"):
-                lax.fori_loop(0, UP_TILES, up_step, 0)
+            @pl.when(n > 0)
+            def _():
+                with jax.named_scope("wait_w2"):
+                    wait_for(w2, local.at[W2_IN])
+                with jax.named_scope("up"):
+                    lax.fori_loop(0, UP_TILES, up_step, 0)
+
             copy(ud, du_hbm.at[n], local.at[DU_OUT]).start()
-
-            @pl.when(n == 0)
-            def _():
-                with jax.named_scope("wait_20"):
-                    ag_wait(2, 0)
-                ag_start(2, 1)
 
             @pl.when(n == nc - 1)
             def _():
@@ -369,6 +400,12 @@
                 for m in range(CHIPS):
                     copy(s1.at[up_rows(k, m, REDUCE)], p1.at[n, k, m], local.at[G1_OUT]).start()
 
+            @pl.when(n == 0)
+            def _():
+                with jax.named_scope("wait_20"):
+                    ag_wait(2, 0)
+                ag_start(2, 1)
+
             @pl.when(n == nc - 2)
             def _():
                 c_add(0)
@@ -390,16 +427,17 @@
         pltpu.VMEM((width, fc), BF16), pltpu.VMEM((fc, width), BF16),
         pltpu.VMEM((both, fc), BF16), pltpu.VMEM((fc, both), BF16),
         pltpu.VMEM((width, fc), BF16), pltpu.VMEM((fc, width), BF16),
-        pltpu.VMEM((4, 3, rows, fc), BF16), pltpu.VMEM((4, 3, units, cols), BF16),
+        pltpu.VMEM((12, rows, fc), BF16), pltpu.VMEM((12, units, cols), BF16),
         pltpu.VMEM((3, 2, rows, fc), BF16), pltpu.VMEM((3, 2, units, cols), BF16))
 
     dx_tile = both // DX_TILES
     half_tiles = DX_TILES // 2
     steps = 3 * DX_TILES
+    own_from = 3 * half_tiles
     hidden = nc * fc
 
-    def last(w, du, out32, out16, got, res,
-             co1, co2, d1, d2, do1, do2, e1, e2, eo1, eo2):
+    def last(w, du, wide, out16, res,
+             co1, co2, do1, do2, e1, e2, eo1, eo2):
         def load_w(n, third_):
             for p in range(8):
                 r, k = divmod(8 * third_ + p, 3)
@@ -437,30 +475,38 @@
             for k in range(COLOURS):
                 rs_start(n, 1, k, to1.at[k], to2.at[k])
 
+        def sum_of(e, k, terms):
+            total = e[k].astype(F32)
+            for i in range(1, terms):
+                total = total + e[3 * i + k].astype(F32)
+            return total.astype(BF16)
+
         def d_load(n):
             with jax.named_scope("wait_rs1"):
                 rs_wait(n, 1)
             for i, (b1, b2) in enumerate(((p1, p2), (ra1, ra2), (rb1, rb2))):
-                copy(b1.at[n, :, 1], d1.at[i], local.at[D_IN]).start()
-                copy(b2.at[n, :, 1], d2.at[i], local.at[D_IN]).start()
+                for k in range(COLOURS):
+                    copy(b1.at[n, k, 1], e1.at[3 * i + k], local.at[D_IN]).start()
+                    copy(b2.at[n, k, 1], e2.at[3 * i + k], local.at[D_IN]).start()
 
         def d_send(n):
-            wait_for(d1, local.at[D_IN])
-            wait_for(d2, local.at[D_IN])
-
-            for k in range(COLOURS):
-                do1[n, k] = (d1[0, k].astype(F32) + d1[1, k].astype(F32) + d1[2, k].astype(F32)).astype(BF16)
-                do2[n, k] = (d2[0, k].astype(F32) + d2[1, k].astype(F32) + d2[2, k].astype(F32)).astype(BF16)
+            wait_for(e1.at[pl.ds(0, 9)], local.at[D_IN])
+            wait_for(e2.at[pl.ds(0, 9)], local.at[D_IN])
+
+            for k in range(COLOURS):
+                do1[n, k] = sum_of(e1, k, 3)
+                do2[n, k] = sum_of(e2, k, 3)
                 rs_start(n, 2, k, do1.at[n, k], do2.at[n, k])
 
         def e_load(n):
             with jax.named_scope("wait_rs2"):
                 rs_wait(n, 2)
             for i, (b1, b2) in enumerate(((p1, p2), (ra1, ra2), (rb1, rb2))):
-                copy(b1.at[n, :, 0], e1.at[i], local.at[E_IN]).start()
-                copy(b2.at[n, :, 0], e2.at[i], local.at[E_IN]).start()
-            copy(rc1.at[n], e1.at[3], local.at[E_IN]).start()
-            copy(rc2.at[n], e2.at[3], local.at[E_IN]).start()
+                for k in range(COLOURS):
+                    copy(b1.at[n, k, 0], e1.at[3 * i + k], local.at[E_IN]).start()
+                    copy(b2.at[n, k, 0], e2.at[3 * i + k], local.at[E_IN]).start()
+            copy(rc1.at[n], e1.at[pl.ds(9, 3)], local.at[E_IN]).start()
+            copy(rc2.at[n], e2.at[pl.ds(9, 3)], local.at[E_IN]).start()
 
         keep = pl.ds(pl.multiple_of(core * half, 16), half)
         give = pl.ds(pl.multiple_of((1 - core) * half, 16), half)
@@ -479,10 +525,8 @@
                 e_wait_out(n - 1)
 
             for k in range(COLOURS):
-                eo1[k * rows:(k + 1) * rows, :] = (
-                    e1[0, k].astype(F32) + e1[1, k].astype(F32) + e1[2, k].astype(F32) + e1[3, k].astype(F32)).astype(BF16)
-                eo2[:, k * cols:(k + 1) * cols] = (
-                    e2[0, k].astype(F32) + e2[1, k].astype(F32) + e2[2, k].astype(F32) + e2[3, k].astype(F32)).astype(BF16)
+                eo1[k * rows:(k + 1) * rows, :] = sum_of(e1, k, 4)
+                eo2[:, k * cols:(k + 1) * cols] = sum_of(e2, k, 4)
             copy(eo1.at[keep], gup_hbm.at[core, n], local.at[GUP_OUT]).start()
             copy(eo2, gdown_hbm.at[pl.ds(pl.multiple_of(n * units, 16), units)], local.at[GDOWN_OUT]).start()
             pltpu.make_async_remote_copy(
@@ -490,17 +534,16 @@
                 device_id=(partner,), device_id_type=MESH).start()
 
         def pump(i):
-            for start, every, low, load, finish_ in (
-                    (0, 2, EARLY, c_in, c_send), (7, 1, 0, d_load, d_send), (15, 1, 0, e_load, e_store)):
-                since = i - start
-
-                @pl.when((since >= 1) & ((since - 1) % every == 0) & ((since - 1) // every < nc - low))
-                def _(finish_=finish_, since=since, every=every, low=low):
-                    finish_((since - 1) // every + low)
-
-                @pl.when((since >= 0) & (since % every == 0) & (since // every < nc - low))
-                def _(load=load, since=since, every=every, low=low):
-                    load(since // every + low)
+            for start, low, load, finish_ in ((0, EARLY, c_in, c_send), (6, 0, d_load, d_send), (15, 0, e_load, e_store)):
+                n = i - start + low
+
+                @pl.when((n > low) & (n <= nc))
+                def _(finish_=finish_, n=n):
+                    finish_(n - 1)
+
+                @pl.when((n >= low) & (n < nc))
+                def _(load=load, n=n):
+                    load(n)
 
         def step(i, carry):
             q, n = i // 3, i % 3
@@ -520,41 +563,47 @@
                 with jax.named_scope("wait_wall"):
                     wait_for(w.at[pl.ds(0, cols)], w_sem.at[n])
 
-            @pl.when((i >= 3 * half_tiles) & (i < steps))
-            def _():
-                here = own_at(q, n)
+            @pl.when((i >= own_from - 1) & (i < steps - 1))
+            def _():
+                here = own_at((i + 1) // 3, (i + 1) % 3)
                 with jax.named_scope("wait_dxr"):
-                    wait_for(dxr_hbm.at[here], dx_recv.at[i - 3 * half_tiles])
-                copy(dxr_hbm.at[here], got, local.at[GOT_IN]).start()
-                copy(dy_hbm.at[here], res, local.at[RES_IN]).start()
-
-            @pl.when((i >= 2) & (i < 3 * half_tiles + 2))
+                    wait_for(dxr_hbm.at[here], dx_recv.at[i + 1 - own_from])
+
+                @pl.when(i < own_from + 2)
+                def _():
+                    wait_for(wide.at[0], dx_send.at[i - 2])
+
+                copy(dxr_hbm.at[here], wide.at[(i + 1) % 3], local.at[GOT_IN + 1 - slot]).start()
+                copy(dy_hbm.at[here], res.at[1 - slot], local.at[RES_IN + 1 - slot]).start()
+
+            @pl.when((i >= 3) & (i < own_from))
             def _():
                 with jax.named_scope("wait_dxs"):
-                    wait_for(out32.at[0], dx_send.at[i - 2])
-
-            @pl.when((i >= 3 * half_tiles + 2) & (i < steps))
+                    wait_for(wide.at[0], dx_send.at[i - 3])
+
+            @pl.when((i >= own_from + 2) & (i < steps))
             def _():
                 wait_for(out16.at[0], local.at[DX_OUT + slot])
 
-            @pl.when(i < steps)
-            def _():
+            def dot():
                 part = pl.ds(pl.multiple_of(n * cols, cols), cols)
+                return lax.dot_general(du[q % 2], w[part, :], (((1,), (1,)), ((), ())), preferred_element_type=F32)
+
+            @pl.when(i < own_from)
+            def _():
                 with jax.named_scope("dx_dot"):
-                    out32[slot] = lax.dot_general(
-                        du[q % 2], w[part, :], (((1,), (1,)), ((), ())), preferred_element_type=F32)
-
-            @pl.when(i < 3 * half_tiles)
-            def _():
+                    wide[i % 3] = dot()
                 pltpu.make_async_remote_copy(
-                    src_ref=out32.at[slot], dst_ref=dxr_hbm.at[own_at(q, n)], send_sem=dx_send.at[i], recv_sem=dx_recv.at[i],
+                    src_ref=wide.at[i % 3], dst_ref=dxr_hbm.at[own_at(q, n)], send_sem=dx_send.at[i], recv_sem=dx_recv.at[i],
                     device_id=(partner,), device_id_type=MESH).start()
 
-            @pl.when((i >= 3 * half_tiles) & (i < steps))
-            def _():
-                wait_for(got, local.at[GOT_IN])
-                wait_for(res, local.at[RES_IN])
-                out16[slot] = (res[...].astype(F32) + (out32[slot] + got[...])).astype(BF16)
+            @pl.when((i >= own_from) & (i < steps))
+            def _():
+                with jax.named_scope("wait_got"):
+                    wait_for(wide.at[0], local.at[GOT_IN + slot])
+                    wait_for(res.at[0], local.at[RES_IN + slot])
+                with jax.named_scope("dx_dot2"):
+                    out16[slot] = (res[slot].astype(F32) + (dot() + wide[i % 3])).astype(BF16)
                 copy(out16.at[slot], dx_hbm.at[own_at(q, n)], local.at[DX_OUT + slot]).start()
 
             pump(i)
@@ -571,12 +620,10 @@
     pl.run_scoped(
         last,
         pltpu.VMEM((width, hidden), BF16), pltpu.VMEM((2, dx_tile, hidden), BF16),
-        pltpu.VMEM((2, dx_tile, cols), F32), pltpu.VMEM((2, dx_tile, cols), BF16),
-        pltpu.VMEM((dx_tile, cols), F32), pltpu.VMEM((dx_tile, cols), BF16),
+        pltpu.VMEM((3, dx_tile, cols), F32), pltpu.VMEM((2, dx_tile, cols), BF16), pltpu.VMEM((2, dx_tile, cols), BF16),
         pltpu.VMEM((nc - EARLY, 3, 2, rows, fc), BF16), pltpu.VMEM((nc - EARLY, 3, 2, units, cols), BF16),
-        pltpu.VMEM((3, 3, rows, fc), BF16), pltpu.VMEM((3, 3, units, cols), BF16),
         pltpu.VMEM((nc, 3, rows, fc), BF16), pltpu.VMEM((nc, 3, units, cols), BF16),
-        pltpu.VMEM((4, 3, rows, fc), BF16), pltpu.VMEM((4, 3, units, cols), BF16),
+        pltpu.VMEM((12, rows, fc), BF16), pltpu.VMEM((12, units, cols), BF16),
         pltpu.VMEM((3 * rows, fc), BF16), pltpu.VMEM((units, width), BF16))
 
     def drain(n, carry):

time: 571 us -> 577 us (1.011)
  Pallas kernels: 570 us -> 576 us
where the time goes in v3:
time: 577 us; the launch traced here: 576 us
  Pallas kernels  576 us (100%)
    pallas_call x1, Pallas kernels, device_fn(): pl.pallas_call(functools.partial(kernel, nc), out_shape=outs, in_specs=[p...  565 us

profile of v3, /device:TPU:0, one launch (start us, length us, event | category | flops | bytes accessed | tf_op | source)
XLA Modules:
  0.0 576.5 jit_solution(4190236707268283286)
XLA Ops:
  0.6 565.3 %shard_map.67 = (bf16[2,9,144,512]{3,2,1,0:T(8,128)(2,1)}, bf16[576,2304]{1,0:T(8,128)(2,1)}, bf16[2048,2304]{1,0:T(8,128)(2,1)}, bf16[2048,2304]{1,0:T(8,128)(2...) custom-call(bf16[2048,2304]{1,0:T(8,128)(2,1)} %bitcast.7, ...), custom_call_target="tpu_custom_call" | custom-call | tf_op jit(solution)/shard_map/pallas_call | solution.py:702
  565.9 10.4 %shard_map.68 = (bf16[144,9216]{1,0:T(8,128)(2,1)}, bf16[576,2304]{1,0:T(8,128)(2,1)}, bf16[2048,2304]{1,0:T(8,128)(2,1)}) custom-call(bf16[2,9,144,512]{3,2,1,0:T(8,128)(2,1)} %get-tuple-element.9.gup, bf16[576,2304]{1,0:T(8,128)(2,1)} %get-tuple-element.10.gdown, bf16[2048,2304]{1,0:T(8,128)(2,1)} %get-tuple-element.11.dx), custom_call_target="tpu_custom_call" | custom-call | tf_op jit(solution)/shard_map/pallas_call | solution.py:715

commit v4 on v3

--- a/solution.py
+++ b/solution.py
@@ -178,20 +178,23 @@
                 send_sem=ag_send.at[1, 0, 0], recv_sem=ag_recv.at[1, 0, 0],
                 device_id=(near[k],), device_id_type=MESH).start()
         wait_for(down_hbm, local.at[X_IN])
-        down_own(0)
-        for n in range(1, nc):
+        for n in range(nc):
+            down_own(n)
+        for n in range(1, 4):
+            permute(n)
+        with jax.named_scope("own_wait"):
+            wait_for(du_hbm.at[0, pl.ds(0, half)], local.at[OWN_0])
+            wait_for(du_hbm.at[0, pl.ds(0, half)], pair_recv.at[0])
+        ag_start(0, 0, (0,))
+        for n in range(4, nc):
             permute(n)
         for n in range(1, nc):
-            down_own(n)
             own_up(n)
         to_partner(x_hbm, xr_hbm, 1)
         to_partner(dy_hbm, dyr_hbm, 2)
-        with jax.named_scope("own_wait"):
-            wait_for(down_hbm.at[pl.ds(0, units)], local.at[X_IN])
-            wait_for(du_hbm.at[0, pl.ds(0, half)], local.at[OWN_0])
-            wait_for(du_hbm.at[0, pl.ds(0, half)], pair_recv.at[0])
-        ag_start(0, 0, (0,))
+        wait_for(down_hbm.at[pl.ds(0, units)], local.at[X_IN])
         wait_for(down_hbm.at[pl.ds(0, (nc - 1) * units)], local.at[OWN_2])
+        ag_start(1, 0, (1,))
         copy(x_hbm, x.at[mine], local.at[X_IN]).start()
         copy(dy_hbm, dy.at[mine], local.at[DY_IN]).start()
         for s in range(2):
@@ -201,7 +204,8 @@
                 ag_start(0, s + 1, (i,))
         wait_for(du_hbm.at[0, pl.ds(0, (nc - 1) * half)], local.at[OWN_1])
         wait_for(du_hbm.at[0, pl.ds(0, (nc - 1) * half)], pair_recv.at[3])
-        ag_start(1, 0)
+        ag_start(1, 0, (0,))
+        ag_start(2, 0)
         with jax.named_scope("xr"):
             wait_for(xr_hbm, pair_recv.at[1])
         copy(xr_hbm, x.at[theirs], local.at[X_IN]).start()
@@ -274,6 +278,19 @@
                 def u_step(t, carry):
                     at_t = pl.ds(pl.multiple_of(t * 2 * up_tile, up_tile), 2 * up_tile)
                     ud[at_t, :] = jnp.dot(x[at_t, :], w1[...], preferred_element_type=F32).astype(BF16)
+
+                    @pl.when(t == 1)
+                    def _():
+                        with jax.named_scope("dyr"):
+                            wait_for(dyr_hbm, pair_recv.at[2])
+                        copy(dyr_hbm, dy.at[theirs], local.at[DY_IN]).start()
+
+                    @pl.when(t == 2)
+                    def _():
+                        with jax.named_scope("ag021"):
+                            ag_wait(0, 2, (1,))
+                        load_down(0)
+
                     return carry
 
                 with jax.named_scope("u0"):
@@ -282,10 +299,6 @@
                     ag_wait(1, 0, (0,))
                 ag_start(1, 1, (0,))
                 with jax.named_scope("first_w2"):
-                    wait_for(dyr_hbm, pair_recv.at[2])
-                    copy(dyr_hbm, dy.at[theirs], local.at[DY_IN]).start()
-                    ag_wait(0, 2, (1,))
-                    load_down(0)
                     wait_for(dy, local.at[DY_IN])
                     wait_for(w2, local.at[W2_IN])
 
@@ -306,7 +319,9 @@
 
                 with jax.named_scope("da0"):
                     lax.fori_loop(0, UP_TILES, da_step, 0)
-                ag_start(2, 0)
+                with jax.named_scope("wait_20"):
+                    ag_wait(2, 0)
+                ag_start(2, 1)
                 ag_start(3, 0)
 
             def up_step(t, carry):
@@ -317,24 +332,15 @@
                     da = da_of(at_t)
                     use(first, lambda r, at_r, lanes, u=u: u[r:r + strip, lanes], da)
 
-                @pl.when(t == 4)
+                @pl.when((t == 2) & (n == 1))
                 def _():
-                    @pl.when(n + 1 < nc)
-                    def _():
-                        with jax.named_scope("wait_ag1"):
-                            ag_wait(n + 1, 1)
-                        ag_start(n + 1, 2)
-
-                    @pl.when(n + 2 < nc)
-                    def _():
-                        with jax.named_scope("wait_ag0"):
-                            ag_wait(n + 2, 0)
-                        ag_start(n + 2, 1)
-
-                    @pl.when(n + 3 < nc)
-                    def _():
-                        ag_start(n + 3, 0)
-
+                    with jax.named_scope("wait_30"):
+                        ag_wait(3, 0)
+                    ag_start(3, 1)
+                    ag_start(4, 0)
+
+                @pl.when(t == 2)
+                def _():
                     send_both(n - 1)
 
                 @pl.when((t == 6) & (n == nc - 1))
@@ -370,6 +376,22 @@
             for k in range(COLOURS):
                 for m in range(CHIPS):
                     copy(s2.at[down_rows(k, m, REDUCE), down_cols(k)], p2.at[n, k, m], local.at[G2_OUT]).start()
+
+            @pl.when((n > 0) & (n + 2 < nc))
+            def _():
+                with jax.named_scope("wait_ag1"):
+                    ag_wait(n + 2, 1)
+                ag_start(n + 2, 2)
+
+            @pl.when((n > 0) & (n + 3 < nc))
+            def _():
+                with jax.named_scope("wait_ag0"):
+                    ag_wait(n + 3, 0)
+                ag_start(n + 3, 1)
+
+            @pl.when((n > 0) & (n + 4 < nc))
+            def _():
+                ag_start(n + 4, 0)
 
             @pl.when(n == nc - 2)
             def _():
@@ -402,9 +424,9 @@
 
             @pl.when(n == 0)
             def _():
-                with jax.named_scope("wait_20"):
-                    ag_wait(2, 0)
-                ag_start(2, 1)
+                with jax.named_scope("wait_21"):
+                    ag_wait(2, 1)
+                ag_start(2, 2)
 
             @pl.when(n == nc - 2)
             def _():
@@ -534,14 +556,15 @@
                 device_id=(partner,), device_id_type=MESH).start()
 
         def pump(i):
-            for start, low, load, finish_ in ((0, EARLY, c_in, c_send), (6, 0, d_load, d_send), (15, 0, e_load, e_store)):
+            for start, low, high, load, finish_ in (
+                    (0, EARLY, nc - 1, c_in, c_send), (8, nc - 1, nc, c_in, c_send), (10, 0, nc, d_load, d_send), (19, 0, nc, e_load, e_store)):
                 n = i - start + low
 
-                @pl.when((n > low) & (n <= nc))
+                @pl.when((n > low) & (n <= high))
                 def _(finish_=finish_, n=n):
                     finish_(n - 1)
 
-                @pl.when((n >= low) & (n < nc))
+                @pl.when((n >= low) & (n < high))
                 def _(load=load, n=n):
                     load(n)
 
@@ -609,7 +632,7 @@
             pump(i)
             return carry
 
-        lax.fori_loop(0, max(steps, nc + 16), step, 0)
+        lax.fori_loop(0, max(steps, nc + 20), step, 0)
         for slot in range(2):
             wait_for(out16.at[0], local.at[DX_OUT + slot])
         e_wait_out(nc - 1)

time: 577 us -> 572 us (level)
  no operation moved by 1% of the time
where the time goes in v4:
time: 572 us
  Pallas kernels  571 us (100%)
    pallas_call x1, Pallas kernels, device_fn(): pl.pallas_call(functools.partial(kernel, nc), out_shape=outs, in_specs=[p...  561 us

profile of v4, /device:TPU:0, one launch (start us, length us, event | category | flops | bytes accessed | tf_op | source)
XLA Modules:
  0.0 571.8 jit_solution(2554860735619268860)
XLA Ops:
  0.6 560.6 %shard_map.67 = (bf16[2,9,144,512]{3,2,1,0:T(8,128)(2,1)}, bf16[576,2304]{1,0:T(8,128)(2,1)}, bf16[2048,2304]{1,0:T(8,128)(2,1)}, bf16[2048,2304]{1,0:T(8,128)(2...) custom-call(bf16[2048,2304]{1,0:T(8,128)(2,1)} %bitcast.7, ...), custom_call_target="tpu_custom_call" | custom-call | tf_op jit(solution)/shard_map/pallas_call | solution.py:725
  561.3 10.4 %shard_map.68 = (bf16[144,9216]{1,0:T(8,128)(2,1)}, bf16[576,2304]{1,0:T(8,128)(2,1)}, bf16[2048,2304]{1,0:T(8,128)(2,1)}) custom-call(bf16[2,9,144,512]{3,2,1,0:T(8,128)(2,1)} %get-tuple-element.9.gup, bf16[576,2304]{1,0:T(8,128)(2,1)} %get-tuple-element.10.gdown, bf16[2048,2304]{1,0:T(8,128)(2,1)} %get-tuple-element.11.dx), custom_call_target="tpu_custom_call" | custom-call | tf_op jit(solution)/shard_map/pallas_call | solution.py:738

commit v5 on v4

--- a/solution.py
+++ b/solution.py
@@ -11,6 +11,8 @@
 MESH = pl.DeviceIdType.MESH
 F32, BF16 = jnp.float32, jnp.bfloat16
 CHIPS, COLOURS, CORES = 8, 3, 2
+CHUNKS = 9
+VMEM_BYTES = 67_000_000
 DX_TILES = 8
 UP_TILES = 8
 PARTS = 2
@@ -50,10 +52,8 @@
 
     tokens, width = x_hbm.shape
     both = 2 * tokens
-    rows = a1.shape[3]
-    fc = a1.shape[4]
-    units = a2.shape[3]
-    cols = a2.shape[4]
+    *_, rows, fc = a1.shape
+    *_, units, cols = a2.shape
     half = up_hbm.shape[0]
     third = half // 3
 
@@ -233,11 +233,10 @@
                     src_ref=src.at[n, k, pl.ds(4, 4)], dst_ref=dst.at[n, k], send_sem=rs_send.at[0, n],
                     recv_sem=rs_recv.at[0, n], device_id=(near[k],), device_id_type=MESH).start()
 
-        def send_both(n):
+        def send_down(n):
+            wait_for(p1.at[0], local.at[G1_OUT])
             wait_for(p2.at[0], local.at[G2_OUT])
             send_first(p2, ra2, n)
-            wait_for(p1.at[0], local.at[G1_OUT])
-            send_first(p1, ra1, n)
 
         def c_in(n):
             c_load(n, c1, c2, local.at[SUM_IN])
@@ -251,6 +250,14 @@
             wait_for(sized[1].at[0], local.at[SUM_OUT])
             for k in range(COLOURS):
                 rs_start(n, 1, k, cb1.at[n, k], cb2.at[n, k])
+
+        def early(slot):
+            if slot > 1:
+                c_go(slot - 2)
+            if 0 < slot <= EARLY:
+                c_add(slot - 1)
+            if slot < EARLY:
+                c_in(slot)
 
         up_tile = both // UP_TILES
 
@@ -341,13 +348,23 @@
 
                 @pl.when(t == 2)
                 def _():
-                    send_both(n - 1)
+                    send_down(n - 1)
+
+                    @pl.when(n > nc - 4)
+                    def _():
+                        send_first(p1, ra1, n - 1)
+
+                    @pl.when((n > 2) & (n < nc - 1))
+                    def _():
+                        send_first(p1, ra1, n - 3)
+
+                @pl.when((t == 6) & (n == nc - 2))
+                def _():
+                    early(0)
 
                 @pl.when((t == 6) & (n == nc - 1))
                 def _():
-                    c_go(0)
-                    c_add(1)
-                    c_in(2)
+                    early(3)
 
                 return carry
 
@@ -362,9 +379,7 @@
 
             @pl.when(n == nc - 1)
             def _():
-                c_go(1)
-                c_add(2)
-                c_in(3)
+                early(4)
 
             def down_grad(k, carry):
                 part = pl.ds(pl.multiple_of(k * cols, cols), cols)
@@ -395,12 +410,11 @@
 
             @pl.when(n == nc - 2)
             def _():
-                c_in(0)
+                early(1)
 
             @pl.when(n == nc - 1)
             def _():
-                c_go(2)
-                c_add(3)
+                early(5)
 
             def up_grad(k, carry):
                 part = pl.ds(pl.multiple_of(k * cols, cols), cols)
@@ -430,18 +444,14 @@
 
             @pl.when(n == nc - 2)
             def _():
-                c_add(0)
-                c_in(1)
-
-            @pl.when(n == nc - 1)
-            def _():
-                c_go(3)
+                early(2)
 
             wait_for(ud, local.at[DU_OUT])
             return carry
 
         lax.fori_loop(0, nc, chunk, 0)
-        send_both(nc - 1)
+        send_down(nc - 1)
+        send_first(p1, ra1, nc - 1)
 
     pl.run_scoped(
         main,
@@ -461,13 +471,14 @@
     def last(w, du, wide, out16, res,
              co1, co2, do1, do2, e1, e2, eo1, eo2):
         def load_w(n, third_):
-            for p in range(8):
-                r, k = divmod(8 * third_ + p, 3)
+            for p in range(CHIPS):
+                piece = CHIPS * third_ + p
+                r, k = divmod(piece, COLOURS)
                 m = 0
                 for i in range(3):
                     d = (k + i) % 3
                     m = m + (1 << i) * ((1 - bits[d]) if (r >> d) & 1 else bits[d])
-                copy(a1.at[n, k, m], w.at[pl.ds((8 * third_ + p) * rows, rows), pl.ds(pl.multiple_of(n * fc, fc), fc)],
+                copy(a1.at[n, k, m], w.at[pl.ds(piece * rows, rows), pl.ds(pl.multiple_of(n * fc, fc), fc)],
                      w_sem.at[third_]).start()
 
         def tokens_at(q):
@@ -480,7 +491,7 @@
             for n in range(nc):
                 copy(du_hbm.at[n, pl.ds(tokens_at(q), dx_tile)], du.at[slot, :, pl.ds(n * fc, fc)], local.at[TILE_IN + slot]).start()
 
-        for third_ in range(3):
+        for third_ in range(COLOURS):
             lax.fori_loop(0, nc, lambda n, carry, third_=third_: (load_w(n, third_), carry)[1], 0)
             if third_ == 0:
                 load_du(0)
@@ -557,7 +568,7 @@
 
         def pump(i):
             for start, low, high, load, finish_ in (
-                    (0, EARLY, nc - 1, c_in, c_send), (8, nc - 1, nc, c_in, c_send), (10, 0, nc, d_load, d_send), (19, 0, nc, e_load, e_store)):
+                    (0, EARLY, nc - 1, c_in, c_send), (7, nc - 1, nc, c_in, c_send), (8, 0, nc, d_load, d_send), (17, 0, nc, e_load, e_store)):
                 n = i - start + low
 
                 @pl.when((n > low) & (n <= high))
@@ -632,7 +643,7 @@
             pump(i)
             return carry
 
-        lax.fori_loop(0, max(steps, nc + 20), step, 0)
+        lax.fori_loop(0, max(steps, nc + 18), step, 0)
         for slot in range(2):
             wait_for(out16.at[0], local.at[DX_OUT + slot])
         e_wait_out(nc - 1)
@@ -691,10 +702,6 @@
         copy(v_dx.at[i], dx_out.at[pl.ds(i * rows, rows)], sem_out.at[i]).wait()
 
 
-def chunks_of(units):
-    return 9 if units % 144 == 0 else 1
-
-
 def solution(mesh):
     def device_fn(x_loc, dy_loc, up_loc, down_loc):
         width = x_loc.shape[-1]
@@ -703,7 +710,7 @@
         tokens = x.shape[0]
         down = down_loc[0]
         half, units_all = up_loc.shape[1], down.shape[0]
-        nc = chunks_of(units_all)
+        nc = CHUNKS
         units = units_all // nc
         fc = CHIPS * units
         rows, cols = 2 * half // 3, width // 3
@@ -732,7 +739,7 @@
                 dma((half_steps,)), dma((half_steps,)), dma((nc,)), dma((nc,)), dma((3,)), dma((13,)),
             ],
             compiler_params=pltpu.CompilerParams(
-                collective_id=0, has_side_effects=True, vmem_limit_bytes=67_000_000),
+                collective_id=0, has_side_effects=True, vmem_limit_bytes=VMEM_BYTES),
         )(x, dy, up, down)
         pieces = 8
         g_up, g_down, dx = pl.pallas_call(
@@ -745,7 +752,7 @@
                 pltpu.VMEM((units_all, width), BF16), pltpu.VMEM((pieces, tokens // pieces, width), BF16),
                 dma((pieces + 2,)), dma((pieces + 2,)),
             ],
-            compiler_params=pltpu.CompilerParams(vmem_limit_bytes=67_000_000),
+            compiler_params=pltpu.CompilerParams(vmem_limit_bytes=VMEM_BYTES),
         )(*got[:3])
         return g_up[None], g_down[None], dx.reshape(x_loc.shape)
 

time: 572 us -> 557 us (0.974)
  Pallas kernels: 571 us -> 556 us
    pallas_call x1, Pallas kernels: 561 us -> 546 us  [device_fn(): pl.pallas_call(functools.partial(kernel, nc), out_shape=outs, in_specs=[p...]
where the time goes in v5:
time: 557 us
  Pallas kernels  556 us (100%)
    pallas_call x1, Pallas kernels, device_fn(): pl.pallas_call(functools.partial(kernel, nc), out_shape=outs, in_specs=[p...  546 us

profile of v5, /device:TPU:0, one launch (start us, length us, event | category | flops | bytes accessed | tf_op | source)
XLA Modules:
  0.0 556.8 jit_solution(16452220064354439431)
XLA Ops:
  0.6 545.6 %shard_map.67 = (bf16[2,9,144,512]{3,2,1,0:T(8,128)(2,1)}, bf16[576,2304]{1,0:T(8,128)(2,1)}, bf16[2048,2304]{1,0:T(8,128)(2,1)}, bf16[2048,2304]{1,0:T(8,128)(2...) custom-call(bf16[2048,2304]{1,0:T(8,128)(2,1)} %bitcast.7, ...), custom_call_target="tpu_custom_call" | custom-call | tf_op jit(solution)/shard_map/pallas_call | solution.py:732
  546.2 10.4 %shard_map.68 = (bf16[144,9216]{1,0:T(8,128)(2,1)}, bf16[576,2304]{1,0:T(8,128)(2,1)}, bf16[2048,2304]{1,0:T(8,128)(2,1)}) custom-call(bf16[2,9,144,512]{3,2,1,0:T(8,128)(2,1)} %get-tuple-element.9.gup, bf16[576,2304]{1,0:T(8,128)(2,1)} %get-tuple-element.10.gdown, bf16[2048,2304]{1,0:T(8,128)(2,1)} %get-tuple-element.11.dx), custom_call_target="tpu_custom_call" | custom-call | tf_op jit(solution)/shard_map/pallas_call | solution.py:745

commit v6 on v5

--- a/solution.py
+++ b/solution.py
@@ -137,6 +137,14 @@
         for b in range(blocks):
             copy(up_hbm.at[:, pl.ds(b * width, width)], x.at[pl.ds(nc * units + b * half, half)], local.at[UP_IN]).start()
         copy(down_hbm, own_down, local.at[X_IN]).start()
+        with jax.named_scope("entry"):
+            pl.semaphore_wait(barrier, 4)
+        for n in range(2):
+            for k in range(COLOURS):
+                pltpu.make_async_remote_copy(
+                    src_ref=down_hbm.at[pl.ds(n * units, units), down_cols(k)], dst_ref=a2.at[n, k, 1],
+                    send_sem=ag_send.at[1, 0, n], recv_sem=ag_recv.at[1, 0, n],
+                    device_id=(near[k],), device_id_type=MESH).start()
         wait_for(up_hbm, local.at[UP_IN])
 
         def unit(chip_, core_, n):
@@ -169,14 +177,7 @@
                 copy(x.at[pl.ds(n * units, units), down_cols(k)], a2.at[n, k, 0], local.at[OWN_2 if n else X_IN]).start()
 
         permute(0)
-        with jax.named_scope("entry"):
-            pl.semaphore_wait(barrier, 4)
         own_up(0)
-        for k in range(COLOURS):
-            pltpu.make_async_remote_copy(
-                src_ref=down_hbm.at[pl.ds(0, units), down_cols(k)], dst_ref=a2.at[0, k, 1],
-                send_sem=ag_send.at[1, 0, 0], recv_sem=ag_recv.at[1, 0, 0],
-                device_id=(near[k],), device_id_type=MESH).start()
         wait_for(down_hbm, local.at[X_IN])
         for n in range(nc):
             down_own(n)
@@ -194,7 +195,6 @@
         to_partner(dy_hbm, dyr_hbm, 2)
         wait_for(down_hbm.at[pl.ds(0, units)], local.at[X_IN])
         wait_for(down_hbm.at[pl.ds(0, (nc - 1) * units)], local.at[OWN_2])
-        ag_start(1, 0, (1,))
         copy(x_hbm, x.at[mine], local.at[X_IN]).start()
         copy(dy_hbm, dy.at[mine], local.at[DY_IN]).start()
         for s in range(2):

time: 557 us -> 557 us (level)
  no operation moved by 1% of the time
where the time goes in v6:
time: 557 us
  Pallas kernels  556 us (100%)
    pallas_call x1, Pallas kernels, device_fn(): pl.pallas_call(functools.partial(kernel, nc), out_shape=outs, in_specs=[p...  546 us

profile of v6, /device:TPU:0, one launch (start us, length us, event | category | flops | bytes accessed | tf_op | source)
XLA Modules:
  0.0 557.0 jit_solution(7845257345476289424)
XLA Ops:
  0.6 545.8 %shard_map.67 = (bf16[2,9,144,512]{3,2,1,0:T(8,128)(2,1)}, bf16[576,2304]{1,0:T(8,128)(2,1)}, bf16[2048,2304]{1,0:T(8,128)(2,1)}, bf16[2048,2304]{1,0:T(8,128)(2...) custom-call(bf16[2048,2304]{1,0:T(8,128)(2,1)} %bitcast.7, ...), custom_call_target="tpu_custom_call" | custom-call | tf_op jit(solution)/shard_map/pallas_call | solution.py:732
  546.5 10.4 %shard_map.68 = (bf16[144,9216]{1,0:T(8,128)(2,1)}, bf16[576,2304]{1,0:T(8,128)(2,1)}, bf16[2048,2304]{1,0:T(8,128)(2,1)}) custom-call(bf16[2,9,144,512]{3,2,1,0:T(8,128)(2,1)} %get-tuple-element.9.gup, bf16[576,2304]{1,0:T(8,128)(2,1)} %get-tuple-element.10.gdown, bf16[2048,2304]{1,0:T(8,128)(2,1)} %get-tuple-element.11.dx), custom_call_target="tpu_custom_call" | custom-call | tf_op jit(solution)/shard_map/pallas_call | solution.py:745

commit v7 on v6

--- a/solution.py
+++ b/solution.py
@@ -139,12 +139,11 @@
         copy(down_hbm, own_down, local.at[X_IN]).start()
         with jax.named_scope("entry"):
             pl.semaphore_wait(barrier, 4)
-        for n in range(2):
-            for k in range(COLOURS):
-                pltpu.make_async_remote_copy(
-                    src_ref=down_hbm.at[pl.ds(n * units, units), down_cols(k)], dst_ref=a2.at[n, k, 1],
-                    send_sem=ag_send.at[1, 0, n], recv_sem=ag_recv.at[1, 0, n],
-                    device_id=(near[k],), device_id_type=MESH).start()
+        for k in range(COLOURS):
+            pltpu.make_async_remote_copy(
+                src_ref=down_hbm.at[pl.ds(0, units), down_cols(k)], dst_ref=a2.at[0, k, 1],
+                send_sem=ag_send.at[1, 0, 0], recv_sem=ag_recv.at[1, 0, 0],
+                device_id=(near[k],), device_id_type=MESH).start()
         wait_for(up_hbm, local.at[UP_IN])
 
         def unit(chip_, core_, n):
@@ -195,8 +194,14 @@
         to_partner(dy_hbm, dyr_hbm, 2)
         wait_for(down_hbm.at[pl.ds(0, units)], local.at[X_IN])
         wait_for(down_hbm.at[pl.ds(0, (nc - 1) * units)], local.at[OWN_2])
+        ag_start(1, 0, (1,))
         copy(x_hbm, x.at[mine], local.at[X_IN]).start()
         copy(dy_hbm, dy.at[mine], local.at[DY_IN]).start()
+        def load_up(n, blocks=range(CHIPS)):
+            for k in range(COLOURS):
+                for m in blocks:
+                    copy(a1.at[n, k, m], w1.at[up_rows(k, m, GATHER)], local.at[W1_IN]).start()
+
         for s in range(2):
             for i in range(2):
                 with jax.named_scope(f"ag0{s}{i}"):
@@ -209,11 +214,7 @@
         with jax.named_scope("xr"):
             wait_for(xr_hbm, pair_recv.at[1])
         copy(xr_hbm, x.at[theirs], local.at[X_IN]).start()
-
-        def load_up(n):
-            for k in range(COLOURS):
-                for m in range(CHIPS):
-                    copy(a1.at[n, k, m], w1.at[up_rows(k, m, GATHER)], local.at[W1_IN]).start()
+        load_up(0, range(4))
 
         def load_down(n):
             for k in range(COLOURS):
@@ -222,7 +223,7 @@
 
         with jax.named_scope("ag020"):
             ag_wait(0, 2, (0,))
-        load_up(0)
+        load_up(0, range(4, CHIPS))
         with jax.named_scope("tokens"):
             wait_for(x, local.at[X_IN])
             wait_for(du_hbm.at[0, pl.ds(0, nc * half)], pair_send.at[0])
@@ -568,7 +569,7 @@
 
         def pump(i):
             for start, low, high, load, finish_ in (
-                    (0, EARLY, nc - 1, c_in, c_send), (7, nc - 1, nc, c_in, c_send), (8, 0, nc, d_load, d_send), (17, 0, nc, e_load, e_store)):
+                    (0, EARLY, nc - 1, c_in, c_send), (6, nc - 1, nc, c_in, c_send), (7, 0, nc, d_load, d_send), (16, 0, nc, e_load, e_store)):
                 n = i - start + low
 
                 @pl.when((n > low) & (n <= high))
@@ -643,7 +644,7 @@
             pump(i)
             return carry
 
-        lax.fori_loop(0, max(steps, nc + 18), step, 0)
+        lax.fori_loop(0, max(steps, nc + 17), step, 0)
         for slot in range(2):
             wait_for(out16.at[0], local.at[DX_OUT + slot])
         e_wait_out(nc - 1)

time: 557 us -> 554 us (level)
  no operation moved by 1% of the time
where the time goes in v7:
time: 554 us
  Pallas kernels  553 us (100%)
    pallas_call x1, Pallas kernels, device_fn(): pl.pallas_call(functools.partial(kernel, nc), out_shape=outs, in_specs=[p...  543 us

profile of v7, /device:TPU:0, one launch (start us, length us, event | category | flops | bytes accessed | tf_op | source)
XLA Modules:
  0.0 553.9 jit_solution(10705676134239018646)
XLA Ops:
  0.6 542.7 %shard_map.67 = (bf16[2,9,144,512]{3,2,1,0:T(8,128)(2,1)}, bf16[576,2304]{1,0:T(8,128)(2,1)}, bf16[2048,2304]{1,0:T(8,128)(2,1)}, bf16[2048,2304]{1,0:T(8,128)(2...) custom-call(bf16[2048,2304]{1,0:T(8,128)(2,1)} %bitcast.7, ...), custom_call_target="tpu_custom_call" | custom-call | tf_op jit(solution)/shard_map/pallas_call | solution.py:733
  543.3 10.4 %shard_map.68 = (bf16[144,9216]{1,0:T(8,128)(2,1)}, bf16[576,2304]{1,0:T(8,128)(2,1)}, bf16[2048,2304]{1,0:T(8,128)(2,1)}) custom-call(bf16[2,9,144,512]{3,2,1,0:T(8,128)(2,1)} %get-tuple-element.9.gup, bf16[576,2304]{1,0:T(8,128)(2,1)} %get-tuple-element.10.gdown, bf16[2048,2304]{1,0:T(8,128)(2,1)} %get-tuple-element.11.dx), custom_call_target="tpu_custom_call" | custom-call | tf_op jit(solution)/shard_map/pallas_call | solution.py:746

commit v8 on v7

--- a/solution.py
+++ b/solution.py
@@ -533,12 +533,12 @@
                 rs_start(n, 2, k, do1.at[n, k], do2.at[n, k])
 
         def e_load(n):
-            with jax.named_scope("wait_rs2"):
-                rs_wait(n, 2)
             for i, (b1, b2) in enumerate(((p1, p2), (ra1, ra2), (rb1, rb2))):
                 for k in range(COLOURS):
                     copy(b1.at[n, k, 0], e1.at[3 * i + k], local.at[E_IN]).start()
                     copy(b2.at[n, k, 0], e2.at[3 * i + k], local.at[E_IN]).start()
+            with jax.named_scope("wait_rs2"):
+                rs_wait(n, 2)
             copy(rc1.at[n], e1.at[pl.ds(9, 3)], local.at[E_IN]).start()
             copy(rc2.at[n], e2.at[pl.ds(9, 3)], local.at[E_IN]).start()
 
@@ -742,7 +742,7 @@
             compiler_params=pltpu.CompilerParams(
                 collective_id=0, has_side_effects=True, vmem_limit_bytes=VMEM_BYTES),
         )(x, dy, up, down)
-        pieces = 8
+        pieces = 16
         g_up, g_down, dx = pl.pallas_call(
             functools.partial(finish, nc, units),
             out_shape=[hbm(half, up.shape[1]), hbm(units_all, width), hbm(tokens, width)],

time: 554 us -> 554 us (level)
  no operation moved by 1% of the time
where the time goes in v8:
time: 554 us
  Pallas kernels  553 us (100%)
    pallas_call x1, Pallas kernels, device_fn(): pl.pallas_call(functools.partial(kernel, nc), out_shape=outs, in_specs=[p...  543 us

profile of v8, /device:TPU:0, one launch (start us, length us, event | category | flops | bytes accessed | tf_op | source)
XLA Modules:
  0.0 553.8 jit_solution(2791167091671077074)
XLA Ops:
  0.6 542.7 %shard_map.67 = (bf16[2,9,144,512]{3,2,1,0:T(8,128)(2,1)}, bf16[576,2304]{1,0:T(8,128)(2,1)}, bf16[2048,2304]{1,0:T(8,128)(2,1)}, bf16[2048,2304]{1,0:T(8,128)(2...) custom-call(bf16[2048,2304]{1,0:T(8,128)(2,1)} %bitcast.7, ...), custom_call_target="tpu_custom_call" | custom-call | tf_op jit(solution)/shard_map/pallas_call | solution.py:733
  543.3 10.3 %shard_map.68 = (bf16[144,9216]{1,0:T(8,128)(2,1)}, bf16[576,2304]{1,0:T(8,128)(2,1)}, bf16[2048,2304]{1,0:T(8,128)(2,1)}) custom-call(bf16[2,9,144,512]{3,2,1,0:T(8,128)(2,1)} %get-tuple-element.9.gup, bf16[576,2304]{1,0:T(8,128)(2,1)} %get-tuple-element.10.gdown, bf16[2048,2304]{1,0:T(8,128)(2,1)} %get-tuple-element.11.dx), custom_call_target="tpu_custom_call" | custom-call | tf_op jit(solution)/shard_map/pallas_call | solution.py:746
